TPU v7x, 8 devices: a whole 2x2x1 slice. The times are simulated.
8 devices in a mesh: dp: 1 (over z), ffn: 2 (over y), emb: 4 (over x, core).
Axes of the slice: x: 2, y: 2, z: 1, core: 2. Of those that a mesh axis runs over, the one named last changes fastest.
Arguments:
- hidden: bfloat16 [4096, 1024], P('dp', 'emb')
- norm_pre: bfloat16 [1024], P('emb')
- norm_post: bfloat16 [1024], P('emb')
- w_router: bfloat16 [1024, 32], P('emb')
- w_gate: bfloat16 [32, 1024, 512], P(None, 'emb', 'ffn')
- w_up: bfloat16 [32, 1024, 512], P(None, 'emb', 'ffn')
- w_down: bfloat16 [32, 512, 1024], P(None, 'ffn', 'emb')
- choice: int32 [4096, 8], P('dp')
Outputs:
- output: bfloat16 [4096, 1024], P('dp', 'emb')
All inputs are finite; a program needn't handle non-finite values.
Results may differ from a plain program's by a relative error of at most 0.0125918.
Values are sent between devices in bfloat16 or wider.
A program may use at most 1 GiB of HBM per device.

v0:
```python
import jax
import jax.numpy as jnp
from jax import lax
from jax.sharding import PartitionSpec as P

EPS = 1e-5


def route_tokens(choice, router_prob, experts, capacity):
    num_tok, top_k = choice.shape
    onehot = (choice[:, :, None] == jnp.arange(experts)[None, None, :]).astype(jnp.int32)
    assigned = jnp.sum(onehot, axis=1)
    before = jnp.cumsum(assigned, axis=0) - assigned
    slot_idx = jnp.sum(onehot * before[:, None, :], axis=2)
    position = jnp.where(slot_idx < capacity, choice * capacity + slot_idx, experts * capacity)
    gate_val = jnp.take_along_axis(router_prob, choice, axis=1)
    flat_pos = position.reshape(-1)
    token_ids = jnp.repeat(jnp.arange(num_tok, dtype=jnp.int32), top_k)
    slot_token = jnp.full((experts * capacity,), num_tok, jnp.int32).at[flat_pos].set(token_ids, mode='drop')
    slot_gate = jnp.zeros((experts * capacity,), jnp.float32).at[flat_pos].set(gate_val.reshape(-1), mode='drop')
    return position, slot_token, slot_gate


def solution(mesh):
    emb_size = mesh.shape['emb']

    def local_block(hidden, norm_pre, norm_post, w_router, w_gate, w_up, w_down, choice):
        num_tok, local_width = hidden.shape
        model_width = local_width * emb_size
        experts = w_gate.shape[0]
        top_k = choice.shape[1]
        capacity = 2 * num_tok * top_k // experts
        hid_f32 = hidden.astype(jnp.float32)
        sq_pre = lax.psum(jnp.sum(hid_f32 * hid_f32, axis=1, keepdims=True), 'emb')
        inv_pre = lax.rsqrt(sq_pre / model_width + EPS)
        normed = (hid_f32 * inv_pre * norm_pre.astype(jnp.float32)).astype(jnp.bfloat16)
        logits = lax.psum(jnp.dot(normed, w_router, preferred_element_type=jnp.float32), 'emb')
        router_prob = jax.nn.softmax(logits, axis=1)
        position, slot_token, slot_gate = route_tokens(choice, router_prob, experts, capacity)
        expert_in = jnp.take(normed, slot_token, axis=0, mode='fill', fill_value=0).reshape(experts, capacity, local_width)
        z_gate = jnp.einsum('ecd,edf->ecf', expert_in, w_gate, preferred_element_type=jnp.float32).astype(jnp.bfloat16)
        z_up = jnp.einsum('ecd,edf->ecf', expert_in, w_up, preferred_element_type=jnp.float32).astype(jnp.bfloat16)
        z_gate, z_up = lax.psum((z_gate, z_up), 'emb')
        act_val = (jax.nn.gelu(z_gate.astype(jnp.float32), approximate=True) * z_up.astype(jnp.float32)).astype(jnp.bfloat16)
        part_out = jnp.einsum('ecf,efd->ecd', act_val, w_down, preferred_element_type=jnp.float32).astype(jnp.bfloat16)
        expert_out = lax.psum(part_out, 'ffn')
        weighted = (expert_out.reshape(experts * capacity, local_width).astype(jnp.float32) * slot_gate[:, None]).astype(jnp.bfloat16)
        picked = jnp.take(weighted, position, axis=0, mode='fill', fill_value=0)
        mix_sum = jnp.sum(picked.astype(jnp.float32), axis=1)
        sq_post = lax.psum(jnp.sum(mix_sum * mix_sum, axis=1, keepdims=True), 'emb')
        inv_post = lax.rsqrt(sq_post / model_width + EPS)
        return (hid_f32 + mix_sum * inv_post * norm_post.astype(jnp.float32)).astype(jnp.bfloat16)

    in_specs = (P('dp', 'emb'), P('emb'), P('emb'), P('emb', None), P(None, 'emb', 'ffn'), P(None, 'emb', 'ffn'), P(None, 'ffn', 'emb'), P('dp', None))
    return jax.shard_map(local_block, mesh=mesh, in_specs=in_specs, out_specs=P('dp', 'emb'), check_vma=False)
```

profile of v0, /device:TPU:0, one launch (start us, length us, event | category | flops | bytes accessed | tf_op | source)
XLA Modules:
  0.0 2939.6 jit_solution(416214876759152671)
XLA Ops:
  6.5 1.6 convert_reduce_fusion.1
  8.2 0.9 copy.27
  9.0 16.3 reduce-window.6
  25.3 0.8 slice_reduce_fusion
  26.3 0.2 broadcast_add_fusion
  26.5 0.3 fusion.22
  26.9 1.7 select_reduce_fusion
  28.6 1.6 compare_and_fusion.1
  30.1 1.9 copy.22
  32.1 2.7 reshape.87
  34.9 1.5 broadcast_in_dim.62
  36.4 2.6 reshape.116
  39.0 120.1 %scatter_custom_fusion = s32[65536]{0:T(1024)S(1)} fusion(s32[32768]{0:T(1024)S(1)} %bitcast.43, s32[32768]{0:T(1024)S(1)} %reshape.116, s32[]{:T(128)} %constant.34.clone.1), kind=kCustom, calls=%fused_computation.55 | custom fusion | bytes 262148 | tf_op jit(solution)/shard_map/scatter | solution.py:19
  159.3 0.6 fusion.18
  160.0 13.1 psum.42
  173.1 1.9 fusion.20
  175.1 256.3 %gather_fusion = bf16[65536,256]{1,0:T(8,128)(2,1)} fusion(bf16[4096,256]{1,0:T(8,128)(2,1)S(1)} %fusion.20, s32[65536]{0:T(1024)S(1)} %fusion.25), kind=kCustom, calls=%fused_computation | custom fusion | bytes 67371008 | tf_op jit(solution)/shard_map/jit(_take)/gather | solution.py:40
  431.4 26.9 fusion.12
  458.3 22.4 fusion.11
  480.8 1.5 fusion.36
  482.3 0.2 all-reduce.5.cloned.1.call-start
  482.5 1091.2 %all-reduce.9.cloned.1.call-done = (bf16[32,2048,256]{2,1,0:T(8,128)(2,1)}, bf16[32,2048,256]{2,1,0:T(8,128)(2,1)}) async-done(((bf16[32,2048,256]{2,1,0:T(8,128)(2,1)}, bf16[32,2048,256]{2,1,0:T(8,128)(2,1)}), (bf16[32,2048,256]{2,1,0:T(8,128)(2,1)}, bf16[32,2048,256]{2,1,0:T(8,128)(2,1)})) %all-reduce.9.cloned.1.call-update) | async-done | bytes 67108880 | tf_op jit(solution)/shard_map/psum | solution.py:43
  1573.8 41.7 %fusion.13 = bf16[32,2048,256]{2,1,0:T(8,128)(2,1)} fusion(bf16[32,256,256]{2,1,0:T(8,128)(2,1)} %param.14, bf16[32,2048,256]{2,1,0:T(8,128)(2,1)} %get-tuple-element.5, bf16[32,2048,256]{2,1,0:T(8,128)(2,1)} %get-tuple-element.6), kind=kOutput, calls=%fused_computation.24 | convolution fusion | flops 8808038400 | bytes 104857600 | tf_op jit(solution)/shard_map/ecf,efd->ecd/dot_general | solution.py:45
  1615.5 0.6 copy-done.16
  1616.1 0.6 convert_element_type.62
  1616.7 1.4 copy.21
  1618.2 0.6 copy.26
  1618.8 1.0 reshape.100
  1619.9 0.6 copy.23
  1620.5 1.0 reshape.106
  1621.5 0.7 broadcast_clamp_fusion
  1622.2 1.1 reduce_max.9
  1623.3 1.1 fusion.24
  1624.4 1.1 fusion.23
  1625.6 260.6 %gather_fusion.2 = f32[32768]{0:T(1024)S(1)} fusion(f32[4096,32]{0,1:T(8,128)S(1)} %fusion.23, s32[32768]{0:T(1024)S(1)} %reshape.106), kind=kCustom, calls=%fused_computation.2 | custom fusion | bytes 524288 | tf_op jit(solution)/shard_map/jit(take_along_axis)/gather | solution.py:16
  1886.2 1.1 reshape.109
  1887.3 0.6 copy.24
  1887.9 0.6 copy.25
  1888.5 1.0 reshape.124
  1889.6 120.6 %scatter_custom_fusion.1 = f32[65536]{0:T(1024)S(1)} fusion(s32[32768]{0:T(1024)} %bitcast.44, f32[32768]{0:T(1024)S(1)} %reshape.124, f32[]{:T(128)} %constant.42.clone.1), kind=kCustom, calls=%fused_computation.53 | custom fusion | bytes 262656 | tf_op jit(solution)/shard_map/scatter | solution.py:20
  2010.2 337.3 %all-reduce.5.cloned.1.call-done = bf16[65536,256]{1,0:T(8,128)(2,1)} async-done(((bf16[65536,256]{1,0:T(8,128)(2,1)}), bf16[65536,256]{1,0:T(8,128)(2,1)}) %all-reduce.5.cloned.1.call-update) | async-done | bytes 33554448 | tf_op jit(solution)/shard_map/psum | solution.py:46
  2347.5 23.1 multiply_convert_fusion
  2370.6 500.6 %gather_fusion.1 = bf16[32768,256]{1,0:T(8,128)(2,1)} fusion(bf16[65536,256]{1,0:T(8,128)(2,1)} %multiply_convert_fusion, s32[32768]{0:T(1024)S(1)} %copy-done.2), kind=kCustom, calls=%fused_computation.1 | custom fusion | bytes 33685504 | tf_op jit(solution)/shard_map/jit(_take)/gather | solution.py:48
  2871.2 45.0 %convert_reduce_fusion = f32[4096,256]{1,0:T(8,128)S(1)} fusion(bf16[32768,256]{1,0:T(8,128)(2,1)} %gather_fusion.1, pred[4096,8]{1,0:T(8,128)(4,1)S(1)} %copy-done.8), kind=kLoop, calls=%fused_computation.17 | loop fusion | flops 24117248 | bytes 21004288 | tf_op jit(solution)/shard_map/reduce_sum | solution.py:49
  2916.2 1.9 copy-done.3
  2918.1 0.6 multiply_reduce_fusion
  2918.8 10.6 psum.47
  2929.4 3.6 fusion.21
  (49 shorter events, 0.9 us)
Async XLA Ops:
  6.5 474.2 %copy-start = (bf16[256,32]{0,1:T(8,128)(2,1)S(1)}, bf16[256,32]{0,1:T(8,128)(2,1)}, u32[]{:S(2)}) copy-start(bf16[256,32]{0,1:T(8,128)(2,1)} %param.11) | copy-start | bytes 49156
  6.5 152.8 %copy-start.15 = (bf16[256]{0:T(256)(128)(2,1)S(1)}, bf16[256]{0:T(256)(128)(2,1)}, u32[]{:S(2)}) copy-start(bf16[256]{0:T(256)(128)(2,1)} %param.9) | copy-start | bytes 1540
  6.5 152.8 %copy-start.4 = (bf16[4096,256]{1,0:T(8,128)(2,1)S(1)}, bf16[4096,256]{1,0:T(8,128)(2,1)}, u32[]{:S(2)}) copy-start(bf16[4096,256]{1,0:T(8,128)(2,1)} %param.8) | copy-start | bytes 6291460
  6.5 1567.2 %all-reduce.9.cloned.1.call-start = ((), (), s32[]{:S(2)}) async-start(), calls=%async_computation.2 | async-start | bytes 134217728 | tf_op jit(solution)/shard_map/psum | solution.py:43
  30.1 8.9 copy-start.9
  34.9 124.3 %copy-start.11 = (s32[32768,1]{0,1:T(1,128)}, s32[32768,1]{0,1:T(1,128)S(1)}, u32[]{:S(2)}) copy-start(s32[32768,1]{0,1:T(1,128)S(1)} %compare_select_fusion) | copy-start | bytes 393220
  431.4 26.9 copy-start.14
  480.7 1141.5 %all-reduce.7.cloned.1.call-start = ((), (), s32[]{:S(2)}) async-start(), calls=%async_computation.1 | async-start | bytes 1048576 | tf_op jit(solution)/shard_map/psum | solution.py:37
  482.3 1865.2 %all-reduce.5.cloned.1.call-start = ((), (), s32[]{:S(2)}) async-start(), calls=%async_computation | async-start | bytes 67108864 | tf_op jit(solution)/shard_map/psum | solution.py:46
  1615.5 0.7 copy-start.16
  1615.5 1.2 copy-start.12
  1615.5 2.6 copy-start.10
  1615.5 4.3 copy-start.6
  1625.6 262.3 %copy-start.7 = (s32[4096,8]{0,1:T(8,128)S(1)}, s32[4096,8]{0,1:T(8,128)}, u32[]{:S(2)}) copy-start(s32[4096,8]{0,1:T(8,128)} %param.15) | copy-start | bytes 393220
  2010.2 360.4 %copy-start.2 = (s32[32768]{0:T(1024)S(1)}, s32[32768]{0:T(1024)}, u32[]{:S(2)}) copy-start(s32[32768]{0:T(1024)} %broadcast_clamp_fusion) | copy-start | bytes 393220
  2370.6 500.7 %copy-start.8 = (pred[4096,8]{1,0:T(8,128)(4,1)S(1)}, pred[4096,8]{1,0:T(8,128)(4,1)}, u32[]{:S(2)}) copy-start(pred[4096,8]{1,0:T(8,128)(4,1)} %copy.21) | copy-start | bytes 98308
  2370.6 562.5 %copy-start.1 = (bf16[256,32]{0,1:T(8,128)(2,1)S(1)}, bf16[256,32]{0,1:T(8,128)(2,1)}, u32[]{:S(2)}) copy-start(bf16[256,32]{0,1:T(8,128)(2,1)} %param.11) | copy-start | bytes 49156
  2871.2 58.2 %copy-start.5 = (bf16[4096,256]{1,0:T(8,128)(2,1)S(1)}, bf16[4096,256]{1,0:T(8,128)(2,1)}, u32[]{:S(2)}) copy-start(bf16[4096,256]{1,0:T(8,128)(2,1)} %param.8) | copy-start | bytes 6291460
  2871.2 58.2 %copy-start.13 = (f32[256]{0:T(256)S(1)}, f32[256]{0:T(256)}, u32[]{:S(2)}) copy-start(f32[256]{0:T(256)} %convert_element_type.62) | copy-start | bytes 3076
  2916.2 1.9 copy-start.3
Sparse Core Ops, SparseCore 0:
  480.8 1092.8 all-reduce.8
  1576.1 27.7 all-reduce.6
  1615.7 731.7 all-reduce.4
where the time goes:
time: 2950 us; the launch traced here: 2940 us
  waiting for transfers between devices  1430 us (48%)
  local copies, waits for them, and re-layouts  1280 us (43%)
  other arithmetic  102 us (3%)
  matrix products  92.6 us (3%)
    psum x1, waiting for transfers between devices, local_block(): z_gate, z_up = lax.psum((z_gate, z_up), 'emb')  1090 us
    gather x1, local copies, waits for them, and re-layouts, local_block(): picked = jnp.take(weighted, position, axis=0, mode='fill', fill_value=0)  501 us
    psum x1, waiting for transfers between devices, local_block(): expert_out = lax.psum(part_out, 'ffn')  337 us
    gather x5, local copies, waits for them, and re-layouts, route_tokens(): gate_val = jnp.take_along_axis(router_prob, choice, axis=1)  264 us
    gather x1, local copies, waits for them, and re-layouts, local_block(): jnp.take(normed, slot_token, axis=0, mode='fill', fill_value=0)  256 us
    scatter x1, local copies, waits for them, and re-layouts, route_tokens(): jnp.zeros((experts * capacity,), jnp.float32).at[flat_pos]  121 us
    scatter x1, local copies, waits for them, and re-layouts, route_tokens(): jnp.full((experts * capacity,), num_tok, jnp.int32).at[flat_pos]  120 us
  transfers between devices with their start and end apart: 3, of which 2 were waited for; matrix products, arithmetic and copies ran while one was open for 15% of the time, Pallas kernels for 0%

commit v1 on v0

v1 whole, which is shorter than its diff:
```python
import functools
import math

import jax
import jax.numpy as jnp
from jax import lax
from jax.experimental import pallas as pl
from jax.experimental.pallas import tpu as pltpu
from jax.sharding import PartitionSpec as P

EPS = 1e-5
LANES = 128
MESH = pl.DeviceIdType.MESH


def gelu_tanh(z):
    return z * (0.5 * (1.0 + jnp.tanh(math.sqrt(2.0 / math.pi) * (z + 0.044715 * (z * z * z)))))


def kernel(
    experts, capacity,
    h_ref, wg_ref, wu_ref, wd_ref, small_ref, choice_ref, out_ref,
    hb, sm, w0, w1, w2, xn, gates, acc, rbuf, ob, gb,
    h_send, h_recv, s_send, s_recv, w_send, w_recv, w_own, f_send, f_recv, r_send, r_recv, o_send, o_recv,
):
    num_tok, lw = h_ref.shape
    fw = wg_ref.shape[2]
    half = num_tok // 2
    quarter = num_tok // 8
    local_e = experts // 4
    tile = 256
    bf16, f32 = jnp.bfloat16, jnp.float32

    f = lax.axis_index("ffn")
    i = lax.axis_index("emb")
    x, c = i // 2, i % 2
    q = 2 * x + f
    sib = 2 * x + (1 - c)

    def chip(d):
        x2 = (x + d // 2) % 2
        f2 = (f + d % 2) % 2
        return x2, f2, 2 * x2 + f2

    def rows(start, size):
        return pl.ds(pl.multiple_of(start, 128), size)

    barrier = pltpu.get_barrier_semaphore()
    for df in range(2):
        for di in range(4):
            if df or di:
                pl.semaphore_signal(
                    barrier, inc=1, device_id={"ffn": (f + df) % 2, "emb": (i + di) % 4}, device_id_type=MESH
                )
    pl.semaphore_wait(barrier, 7)

    def remote(src, dst, send, recv, f2, i2):
        return pltpu.make_async_remote_copy(
            src_ref=src, dst_ref=dst, send_sem=send, recv_sem=recv,
            device_id={"ffn": f2, "emb": i2}, device_id_type=MESH,
        )

    def await_bytes(ref, sem):
        pltpu.make_async_copy(ref, ref, sem).wait()

    own_h = pltpu.make_async_copy(h_ref.at[rows(c * half, half), :], hb.at[i], h_recv.at[i])
    own_s = pltpu.make_async_copy(small_ref, sm.at[i], s_recv.at[i])
    own_h.start()
    own_s.start()
    peers = [(sib, 1 - c)] + [(2 * (1 - x) + c2, c2) for c2 in range(2)]
    for n, (i2, c2) in enumerate(peers):
        remote(small_ref, sm.at[i], s_send.at[n], s_recv.at[i], f, i2).start()
        remote(h_ref.at[rows(c2 * half, half), :], hb.at[i], h_send.at[n], h_recv.at[i], f, i2).start()

    def blocks(j, fs, es):
        return (
            w0.at[j, fs, rows(es * lw, lw), :],
            w1.at[j, fs, rows(es * lw, lw), :],
            w2.at[j, es, rows(fs * fw, fw), :],
        )

    def group(j):
        return w0.at[j, 0, pl.ds(0, 3 * lw), :]

    def send_expert(j):
        dst = blocks(j, f, i)
        e = local_e * q + j
        for src, to in zip((wg_ref.at[e], wu_ref.at[e], wd_ref.at[e]), dst):
            pltpu.make_async_copy(src, to, w_own.at[j]).start()
            remote(src, to, f_send.at[j, 0], f_recv.at[j, 0], f, sib).start()
        for d in (3, 2, 1):
            x2, f2, q2 = chip(d)
            e2 = local_e * q2 + j
            for src, to in zip((wg_ref.at[e2], wu_ref.at[e2], wd_ref.at[e2]), dst):
                remote(src, to, w_send.at[j, d - 1], w_recv.at[j, d - 1], f2, 2 * x2 + c).start()

    ahead = 4
    for j in range(ahead):
        send_expert(j)

    lane = lax.broadcasted_iota(jnp.int32, (tile, LANES), 1)

    def chosen(start):
        ch = choice_ref[rows(start, tile), :]
        a = jnp.zeros((tile, LANES), f32)
        for k in range(choice_ref.shape[1]):
            a = a + jnp.where(ch[:, k : k + 1] == lane, 1.0, 0.0)
        return a

    def count(n, total):
        return total + jnp.sum(chosen(n * tile), axis=0, keepdims=True)

    first = lax.fori_loop(0, half // tile, count, jnp.zeros((1, LANES), f32))
    strict = lax.broadcasted_iota(jnp.int32, (tile, tile), 0) > lax.broadcasted_iota(jnp.int32, (tile, tile), 1)
    strict = jnp.where(strict, 1.0, 0.0).astype(bf16)

    def place(n, carry):
        a = chosen(c * half + n * tile)
        before = carry + jnp.dot(strict, a.astype(bf16), preferred_element_type=f32)
        gates[rows(n * tile, tile), :] = jnp.where(before < capacity, a, 0.0)
        acc[rows(n * tile, tile), :] = jnp.zeros((tile, acc.shape[1]), f32)
        return carry + jnp.sum(a, axis=0, keepdims=True)

    lax.fori_loop(0, half // tile, place, first * c.astype(f32))

    for b in range(4):
        await_bytes(sm.at[b], s_recv.at[b])
        await_bytes(hb.at[b], h_recv.at[b])

    def route(n, _):
        r = rows(n * tile, tile)
        sq = jnp.zeros((tile, 1), f32)
        for b in range(4):
            hv = hb[b, r, :].astype(f32)
            sq = sq + jnp.sum(hv * hv, axis=1, keepdims=True)
        inv = lax.rsqrt(sq / (4 * lw) + EPS)
        logits = jnp.zeros((tile, LANES), f32)
        for b in range(4):
            normed = (hb[b, r, :].astype(f32) * inv * sm[b, LANES : LANES + 1, :].astype(f32)).astype(bf16)
            xn[r, b * lw : (b + 1) * lw] = normed
            logits = logits + lax.dot_general(
                normed, sm[b, 0:LANES, :], (((1,), (1,)), ((), ())), preferred_element_type=f32
            )
        logits = jnp.where(lane < experts, logits, -jnp.inf)
        p = jnp.exp(logits - jnp.max(logits, axis=1, keepdims=True))
        p = p / jnp.sum(p, axis=1, keepdims=True)
        gates[r, :] = jnp.where(gates[r, :] > 0.0, p, 0.0)
        return 0

    lax.fori_loop(0, half // tile, route, 0)

    lane_q = lax.broadcasted_iota(jnp.int32, (quarter, LANES), 1)

    def expert(j, _):
        @pl.when(j + ahead < local_e)
        def _():
            send_expert(j + ahead)

        await_bytes(group(j), w_own.at[j])
        for d in (1, 2, 3):
            x2, f2, _q2 = chip(d)
            await_bytes(group(j), w_recv.at[j, d - 1])
            for ref in blocks(j, f2, 2 * x2 + c):
                remote(ref, ref, f_send.at[j, d], f_recv.at[j, d], f, sib).start()
        for d in range(4):
            await_bytes(group(j), f_recv.at[j, d])

        def step(n, _):
            d = (n + 1) % 4
            x2, f2, q2 = chip(d)
            r = rows(q2 * quarter, quarter)
            gate = jnp.sum(jnp.where(lane_q == local_e * q + j, gates[r, :], 0.0), axis=1, keepdims=True)
            for s in range(2):
                z0 = jnp.dot(xn[r, :], w0[j, s], preferred_element_type=f32).astype(bf16).astype(f32)
                z1 = jnp.dot(xn[r, :], w1[j, s], preferred_element_type=f32).astype(bf16).astype(f32)
                g = jnp.where(gate > 0.0, gelu_tanh(z0) * z1, 0.0)
                gb[:, s * fw : (s + 1) * fw] = g.astype(bf16)
            for b in range(4):
                y = jnp.dot(gb[...], w2[j, b], preferred_element_type=f32).astype(bf16).astype(f32)
                u = (y * gate).astype(bf16).astype(f32)
                acc[r, b * lw : (b + 1) * lw] += u

            @pl.when((j == local_e - 1) & (d > 0))
            def _():
                remote(
                    acc.at[r, :], rbuf.at[d - 1], r_send.at[d - 1], r_recv.at[d - 1], f2, 2 * x2 + c
                ).start()

            return 0

        lax.fori_loop(0, 4, step, 0)
        return 0

    lax.fori_loop(0, local_e, expert, 0)

    for d in (1, 2, 3):
        await_bytes(rbuf.at[d - 1], r_recv.at[d - 1])
    part = 128

    def finish(n, _):
        r = rows(q * quarter + n * part, part)
        s = rows(n * part, part)
        m = []
        sq = jnp.zeros((part, 1), f32)
        for b in range(4):
            cols = slice(b * lw, (b + 1) * lw)
            v = (acc[r, cols] + rbuf[0, s, cols]) + (rbuf[1, s, cols] + rbuf[2, s, cols])
            sq = sq + jnp.sum(v * v, axis=1, keepdims=True)
            m.append(v)
        inv = lax.rsqrt(sq / (4 * lw) + EPS)
        for b in range(4):
            post = sm[b, LANES + 1 : LANES + 2, :].astype(f32)
            ob[b, s, :] = (hb[b, r, :].astype(f32) + m[b] * inv * post).astype(bf16)
        return 0

    lax.fori_loop(0, quarter // part, finish, 0)

    mine = out_ref.at[rows(c * half + q * quarter, quarter), :]
    me = 4 * f + i
    for df in range(2):
        for di in range(4):
            f2, i2 = (f + df) % 2, (i + di) % 4
            if df or di:
                remote(ob.at[i2], mine, o_send.at[4 * df + di], o_recv.at[me], f2, i2).start()
            else:
                pltpu.make_async_copy(ob.at[i], mine, o_send.at[0]).start()
    for df in range(2):
        for di in range(4):
            if df or di:
                await_bytes(ob.at[0], o_recv.at[4 * ((f + df) % 2) + (i + di) % 4])
            await_bytes(ob.at[0], o_send.at[4 * df + di])

    for n in range(3):
        await_bytes(sm.at[0], s_send.at[n])
        await_bytes(hb.at[0], h_send.at[n])
        await_bytes(rbuf.at[0], r_send.at[n])

    def drain(j, _):
        for d in range(4):
            await_bytes(group(j), f_send.at[j, d])
            if d:
                await_bytes(group(j), w_send.at[j, d - 1])
        return 0

    lax.fori_loop(0, local_e, drain, 0)


def solution(mesh):
    emb_size = mesh.shape["emb"]
    ffn_size = mesh.shape["ffn"]
    assert emb_size == 4 and ffn_size == 2

    def local_block(hidden, norm_pre, norm_post, w_router, w_gate, w_up, w_down, choice):
        num_tok, lw = hidden.shape
        experts, _, fw = w_gate.shape
        top_k = choice.shape[1]
        capacity = 2 * num_tok * top_k // experts
        width, ffn = lw * emb_size, fw * ffn_size
        half, quarter, local_e = num_tok // 2, num_tok // 8, experts // 4
        small_rows = LANES + 16
        small = jnp.concatenate([
            jnp.pad(w_router.T, ((0, LANES - experts), (0, 0))),
            norm_pre[None, :],
            norm_post[None, :],
            jnp.zeros((14, lw), jnp.bfloat16),
        ])
        bf16, f32 = jnp.bfloat16, jnp.float32
        dma = pltpu.SemaphoreType.DMA
        anywhere = pl.BlockSpec(memory_space=pl.ANY)
        flops = 2 * 3 * half * local_e * width * ffn
        return pl.pallas_call(
            functools.partial(kernel, experts, capacity),
            out_shape=jax.ShapeDtypeStruct((num_tok, lw), bf16),
            in_specs=[anywhere] * 5 + [pl.BlockSpec(memory_space=pltpu.VMEM)],
            out_specs=anywhere,
            scratch_shapes=[
                pltpu.VMEM((4, half, lw), bf16),
                pltpu.VMEM((4, small_rows, lw), bf16),
                pltpu.VMEM((local_e, 2, width, fw), bf16),
                pltpu.VMEM((local_e, 2, width, fw), bf16),
                pltpu.VMEM((local_e, 4, ffn, lw), bf16),
                pltpu.VMEM((half, width), bf16),
                pltpu.VMEM((half, LANES), f32),
                pltpu.VMEM((half, width), f32),
                pltpu.VMEM((3, quarter, width), f32),
                pltpu.VMEM((4, quarter, lw), bf16),
                pltpu.VMEM((quarter, ffn), bf16),
                dma((3,)), dma((4,)), dma((3,)), dma((4,)),
                dma((local_e, 3)), dma((local_e, 3)), dma((local_e,)),
                dma((local_e, 4)), dma((local_e, 4)),
                dma((3,)), dma((3,)), dma((8,)), dma((8,)),
            ],
            compiler_params=pltpu.CompilerParams(
                collective_id=0, has_side_effects=True, vmem_limit_bytes=67043328
            ),
            cost_estimate=pl.CostEstimate(flops=flops, bytes_accessed=60 << 20, transcendentals=half * local_e * ffn),
        )(hidden, w_gate, w_up, w_down, small, choice)

    in_specs = (P('dp', 'emb'), P('emb'), P('emb'), P('emb', None), P(None, 'emb', 'ffn'), P(None, 'emb', 'ffn'), P(None, 'ffn', 'emb'), P('dp', None))
    return jax.shard_map(local_block, mesh=mesh, in_specs=in_specs, out_specs=P('dp', 'emb'), check_vma=False)
```

time: 2950 us -> 324 us (0.11)
  waiting for transfers between devices: 1430 us -> 0 us
  local copies, waits for them, and re-layouts: 1280 us -> 7.27 us
  Pallas kernels: 0 us -> 314 us
  other arithmetic: 102 us -> 1.44 us
  matrix products: 92.6 us -> 0 us
    psum x3 -> x0, waiting for transfers between devices: 1430 us -> none  [the longest x1 1090 us: local_block(): z_gate, z_up = lax.psum((z_gate, z_up), 'emb')]
    gather x7 -> x0, local copies, waits for them, and re-layouts: 1020 us -> none  [the longest x1 501 us: local_block(): picked = jnp.take(weighted, position, axis=0, mode='fill', fill_value=0)]
    pallas_call x0 -> x1, Pallas kernels: none -> 314 us  [local_block(): pl.pallas_call(functools.partial(kernel, experts, capacity), out_shape=ja...]
    scatter x2 -> x0, local copies, waits for them, and re-layouts: 241 us -> none  [the longest x1 121 us: route_tokens(): jnp.zeros((experts * capacity,), jnp.float32).at[flat_pos]]
    dot_general x4 -> x0, matrix products: 92.6 us -> none  [the longest x1 41.7 us: local_block(): jnp.einsum('ecf,efd->ecd', act_val, w_down, preferred_element_type=jnp.fl...]
    reduce_sum x6 -> x0, other arithmetic: 50.7 us -> none  [the longest x1 45 us: local_block(): mix_sum = jnp.sum(picked.astype(jnp.float32), axis=1)]
  transfers between devices with their start and end apart: 3 -> 0, of which waited for: 2 -> 0; matrix products, arithmetic and copies ran while one was open for 15% -> 0% of each run, Pallas kernels for 0% -> 0%
where the time goes in v1:
time: 324 us; the launch traced here: 323 us
  Pallas kernels  314 us (97%)
  local copies, waits for them, and re-layouts  7.27 us (2%)
    pallas_call x1, Pallas kernels, local_block(): pl.pallas_call(functools.partial(kernel, experts, capacity), out_shape=ja...  314 us

profile of v1, /device:TPU:0, one launch (start us, length us, event | category | flops | bytes accessed | tf_op | source)
XLA Modules:
  0.0 323.0 jit_solution(1996473923574660280)
XLA Ops:
  0.0 0.1 pad.8.clone
  0.1 0.7 broadcast_in_dim.9
  0.7 0.7 broadcast_in_dim.10
  1.4 1.4 fusion.3.small_ref
  2.8 2.8 copy.9.choice_ref
  5.7 314.2 %shard_map.82 = bf16[4096,256]{1,0:T(8,128)(2,1)} custom-call(bf16[4096,256]{1,0:T(8,128)(2,1)} %h_ref.1, bf16[32,256,256]{2,1,0:T(8,128)(2,1)} %wg_ref.1, bf16[32,256,256]{2,1,0:T(8,128)(2,1)} %wu_ref.1, bf16[32,256,256]{2,1,0:T(8,128)(2,1)} %wd_ref.1, bf16[144,256]{1,0:T(8,128)(2,1)} %fusion.3.small_ref, s32[4096,8]{1,0:T(8,128)} %copy.9.choice_ref), custom_call_target="tpu_custom_call" | custom-call | flops 51539607552 | bytes 62914560 | tf_op jit(solution)/shard_map/pallas_call | solution.py:271
  319.9 3.0 copy.11
  (1 shorter events, 0.0 us)

commit v2 on v1

v2 whole, which is shorter than its diff:
```python
import functools
import math

import jax
import jax.numpy as jnp
from jax import lax
from jax.experimental import pallas as pl
from jax.experimental.pallas import tpu as pltpu
from jax.sharding import PartitionSpec as P

EPS = 1e-5
LANES = 128
MESH = pl.DeviceIdType.MESH


def gelu_tanh(z):
    return z * (0.5 * (1.0 + jnp.tanh(math.sqrt(2.0 / math.pi) * (z + 0.044715 * (z * z * z)))))


def kernel(
    experts, capacity,
    h_ref, wg_ref, wu_ref, wd_ref, small_ref, choice_ref, out_ref,
    hb, sm, w0, w1, w2, xn, gates, acc, ybuf, xbuf, ob, gb,
    h_send, h_recv, hf_send, hf_recv, s_send, s_recv, w_send, w_recv, w_own, f_send, f_recv,
    y_send, y_recv, x_send, x_recv, o_send, o_recv,
):
    num_tok, lw = h_ref.shape
    fw = wg_ref.shape[2]
    half = num_tok // 2
    quarter = num_tok // 8
    local_e = experts // 4
    tile = 256
    parts = y_recv.shape[1]
    part = quarter // parts
    cut = ybuf.shape[2]
    bf16, f32 = jnp.bfloat16, jnp.float32

    f = lax.axis_index("ffn")
    i = lax.axis_index("emb")
    x, c = i // 2, i % 2
    q = 2 * x + f
    sib = 2 * x + (1 - c)

    def chip(d):
        x2 = (x + d // 2) % 2
        f2 = (f + d % 2) % 2
        return x2, f2, 2 * x2 + f2

    def rows(start, size):
        return pl.ds(pl.multiple_of(start, 128), size)

    barrier = pltpu.get_barrier_semaphore()
    for df in range(2):
        for di in range(4):
            if df or di:
                pl.semaphore_signal(
                    barrier, inc=1, device_id={"ffn": (f + df) % 2, "emb": (i + di) % 4}, device_id_type=MESH
                )
    pl.semaphore_wait(barrier, 7)

    def remote(src, dst, send, recv, f2, i2):
        return pltpu.make_async_remote_copy(
            src_ref=src, dst_ref=dst, send_sem=send, recv_sem=recv,
            device_id={"ffn": f2, "emb": i2}, device_id_type=MESH,
        )

    def await_bytes(ref, sem):
        pltpu.make_async_copy(ref, ref, sem).wait()

    own_h = pltpu.make_async_copy(h_ref.at[rows(c * half, half), :], hb.at[i], h_recv.at[i])
    own_s = pltpu.make_async_copy(small_ref, sm.at[i], s_recv.at[i])
    own_h.start()
    own_s.start()
    across = rows(f * (half // 2), half // 2)
    far = rows((1 - f) * (half // 2), half // 2)
    for c2 in range(2):
        i2 = 2 * (1 - x) + c2
        remote(small_ref, sm.at[i], s_send.at[c2], s_recv.at[i], f, i2).start()
        src = h_ref.at[rows(c2 * half + f * (half // 2), half // 2), :]
        remote(src, hb.at[i, across, :], h_send.at[c2], h_recv.at[i], f, i2).start()
    remote(small_ref, sm.at[i], s_send.at[2], s_recv.at[i], f, sib).start()
    remote(h_ref.at[rows((1 - c) * half, half), :], hb.at[i], h_send.at[2], h_recv.at[i], f, sib).start()

    def blocks(j, fs, es):
        return (
            w0.at[j, fs, rows(es * lw, lw), :],
            w1.at[j, fs, rows(es * lw, lw), :],
            w2.at[j, es, rows(fs * fw, fw), :],
        )

    def group(j):
        return w0.at[j, 0, pl.ds(0, 3 * lw), :]

    def send_expert(j):
        dst = blocks(j, f, i)
        e = local_e * q + j
        for src, to in zip((wg_ref.at[e], wu_ref.at[e], wd_ref.at[e]), dst):
            pltpu.make_async_copy(src, to, w_own.at[j]).start()
            remote(src, to, f_send.at[j, 0], f_recv.at[j, 0], f, sib).start()
        for d in (3, 2, 1):
            x2, f2, q2 = chip(d)
            e2 = local_e * q2 + j
            for src, to in zip((wg_ref.at[e2], wu_ref.at[e2], wd_ref.at[e2]), dst):
                remote(src, to, w_send.at[j, d - 1], w_recv.at[j, d - 1], f2, 2 * x2 + c).start()

    ahead = 4
    for j in range(2):
        send_expert(j)

    sublane = lax.broadcasted_iota(jnp.int32, (experts, tile), 0)

    def chosen(start):
        ch = choice_ref[:, pl.ds(pl.multiple_of(start, LANES), tile)]
        a = jnp.zeros((experts, tile), f32)
        for k in range(choice_ref.shape[0]):
            a = a + jnp.where(ch[k : k + 1, :] == sublane, 1.0, 0.0)
        return a

    def count(n, total):
        return total + jnp.sum(chosen(n * tile), axis=1, keepdims=True)

    first = lax.fori_loop(0, half // tile, count, jnp.zeros((experts, 1), f32))
    strict = lax.broadcasted_iota(jnp.int32, (tile, tile), 0) < lax.broadcasted_iota(jnp.int32, (tile, tile), 1)
    strict = jnp.where(strict, 1.0, 0.0).astype(bf16)

    def place(n, carry):
        a = chosen(c * half + n * tile)
        before = carry + jnp.dot(a.astype(bf16), strict, preferred_element_type=f32)
        gates[rows(n * tile, tile), :] = jnp.where(before < capacity, a, 0.0).T
        acc[rows(n * tile, tile), :] = jnp.zeros((tile, acc.shape[1]), f32)
        return carry + jnp.sum(a, axis=1, keepdims=True)

    lax.fori_loop(0, half // tile, place, first * c.astype(f32))

    for c2 in range(2):
        e2 = 2 * (1 - x) + c2
        await_bytes(hb.at[e2, across, :], h_recv.at[e2])
        ref = hb.at[e2, across, :]
        remote(ref, ref, hf_send.at[c2], hf_recv.at[c2], 1 - f, i).start()
    for j in range(2, ahead):
        send_expert(j)
    for c2 in range(2):
        await_bytes(hb.at[2 * x + c2], h_recv.at[2 * x + c2])
        await_bytes(hb.at[2 * (1 - x) + c2, far, :], hf_recv.at[c2])
    for b in range(4):
        await_bytes(sm.at[b], s_recv.at[b])

    def route(n, _):
        r = rows(n * tile, tile)
        sq = jnp.zeros((tile, 1), f32)
        for b in range(4):
            hv = hb[b, r, :].astype(f32)
            sq = sq + jnp.sum(hv * hv, axis=1, keepdims=True)
        inv = lax.rsqrt(sq / (4 * lw) + EPS)
        logits = jnp.zeros((tile, experts), f32)
        for b in range(4):
            normed = (hb[b, r, :].astype(f32) * inv * sm[b, experts : experts + 1, :].astype(f32)).astype(bf16)
            xn[r, b * lw : (b + 1) * lw] = normed
            logits = logits + lax.dot_general(
                normed, sm[b, 0:experts, :], (((1,), (1,)), ((), ())), preferred_element_type=f32
            )
        p = jnp.exp(logits - jnp.max(logits, axis=1, keepdims=True))
        p = p / jnp.sum(p, axis=1, keepdims=True)
        gates[r, :] = jnp.where(gates[r, :] > 0.0, p, 0.0)
        return 0

    lax.fori_loop(0, half // tile, route, 0)

    def to_y(src, slot, t):
        return remote(
            src, ybuf.at[slot, rows(t * part, part), :], y_send.at[slot, t], y_recv.at[slot, t], 1 - f, i
        )

    def to_x(src, slot, t):
        return remote(
            src, xbuf.at[slot, rows(t * part, part), :], x_send.at[slot, t], x_recv.at[slot, t], f, 2 * (1 - x) + c
        )

    def y_to_x(src, t):
        return remote(
            src, ybuf.at[2, rows(t * part, part), :], y_send.at[2, t], y_recv.at[2, t], f, 2 * (1 - x) + c
        )

    def x_to_y(src, t):
        return remote(src, xbuf.at[2, rows(t * part, part), :], x_send.at[2, t], x_recv.at[2, t], 1 - f, i)

    def out_rows(xs, fs, cs, t):
        return rows(cs * half + (2 * xs + fs) * quarter + t * part, part)

    lane_q = lax.broadcasted_iota(jnp.int32, (quarter, experts), 1)

    def expert(j, _):
        @pl.when(j + ahead < local_e)
        def _():
            send_expert(j + ahead)

        await_bytes(group(j), w_own.at[j])
        for d in (1, 2, 3):
            x2, f2, _q2 = chip(d)
            await_bytes(group(j), w_recv.at[j, d - 1])
            for ref in blocks(j, f2, 2 * x2 + c):
                remote(ref, ref, f_send.at[j, d], f_recv.at[j, d], f, sib).start()
        for d in range(4):
            await_bytes(group(j), f_recv.at[j, d])

        def step(n, _):
            x2 = (x + n + 1) % 2
            f2 = (f + 1 - n // 2) % 2
            r = rows((2 * x2 + f2) * quarter, quarter)
            gate = jnp.sum(jnp.where(lane_q == local_e * q + j, gates[r, :], 0.0), axis=1, keepdims=True)
            for s in range(2):
                z0 = jnp.dot(xn[r, :], w0[j, s], preferred_element_type=f32).astype(bf16).astype(f32)
                z1 = jnp.dot(xn[r, :], w1[j, s], preferred_element_type=f32).astype(bf16).astype(f32)
                g = jnp.where(gate > 0.0, gelu_tanh(z0) * z1, 0.0)
                gb[:, s * fw : (s + 1) * fw] = g.astype(bf16)
            for b in range(4):
                y = jnp.dot(gb[...], w2[j, b], preferred_element_type=f32).astype(bf16).astype(f32)
                u = (y * gate).astype(bf16).astype(f32)
                acc[r, b * lw : (b + 1) * lw] += u

            start = (2 * x2 + f2) * quarter

            @pl.when((j == local_e - 1) & (n < 2))
            def _():
                for t in range(parts):
                    src = acc.at[rows(start + t * part, part), 0:cut]
                    to_y(src, n, t).start()

            @pl.when((j == local_e - 1) & (n % 2 == 0) & (n < 3))
            def _():
                for t in range(parts):
                    src = acc.at[rows(start + t * part, part), cut:]
                    to_x(src, n // 2, t).start()

            return 0

        lax.fori_loop(0, 4, step, 0)
        return 0

    lax.fori_loop(0, local_e, expert, 0)

    def mid(t, _):
        xr = rows((2 * (1 - x) + f) * quarter + t * part, part)
        yr = rows((2 * x + 1 - f) * quarter + t * part, part)
        buf = rows(t * part, part)
        await_bytes(xbuf.at[0, buf, :], x_recv.at[0, t])
        acc[yr, cut:] = acc[yr, cut:] + xbuf[0, buf, :]
        x_to_y(acc.at[yr, cut:], t).start()
        await_bytes(ybuf.at[0, buf, :], y_recv.at[0, t])
        acc[xr, 0:cut] = acc[xr, 0:cut] + ybuf[0, buf, :]
        y_to_x(acc.at[xr, 0:cut], t).start()
        return 0

    lax.fori_loop(0, parts, mid, 0)

    step_rows = 128

    def finish(t, _):
        buf = rows(t * part, part)
        for n in (1, 2):
            await_bytes(ybuf.at[n, buf, :], y_recv.at[n, t])
            await_bytes(xbuf.at[n, buf, :], x_recv.at[n, t])

        def norm(n, _):
            r = rows(q * quarter + t * part + n * step_rows, step_rows)
            s = rows(t * part + n * step_rows, step_rows)
            lo = acc[r, 0:cut] + (ybuf[1, s, :] + ybuf[2, s, :])
            hi = acc[r, cut:] + (xbuf[1, s, :] + xbuf[2, s, :])
            sq = jnp.sum(lo * lo, axis=1, keepdims=True) + jnp.sum(hi * hi, axis=1, keepdims=True)
            inv = lax.rsqrt(sq / (4 * lw) + EPS)
            acc[r, 0:cut] = lo * inv
            acc[r, cut:] = hi * inv
            for b in range(4):
                post = sm[b, experts + 1 : experts + 2, :].astype(f32)
                ob[b, s, :] = (hb[b, r, :].astype(f32) + acc[r, b * lw : (b + 1) * lw] * post).astype(bf16)
            return 0

        lax.fori_loop(0, part // step_rows, norm, 0)

        mine = out_ref.at[out_rows(x, f, c, t), :]
        for c2 in range(2):
            i2 = 2 * (1 - x) + c2
            remote(ob.at[i2, buf, :], mine, o_send.at[2 + c2, t], o_recv.at[1 + c, t], f, i2).start()
        for c2 in range(2):
            i2 = 2 * x + c2
            remote(ob.at[i2, buf, :], mine, o_send.at[4 + c2, t], o_recv.at[3 + c, t], 1 - f, i2).start()
        pltpu.make_async_copy(ob.at[i, buf, :], mine, o_send.at[0, t]).start()
        remote(ob.at[sib, buf, :], mine, o_send.at[1, t], o_recv.at[0, t], f, sib).start()
        return 0

    lax.fori_loop(0, parts, finish, 0)

    def pass_on(t, _):
        for c2 in range(2):
            there = out_ref.at[out_rows(1 - x, f, c2, t), :]
            await_bytes(there, o_recv.at[1 + c2, t])
            remote(there, there, o_send.at[6 + c2, t], o_recv.at[5 + c2, t], 1 - f, i).start()
        return 0

    lax.fori_loop(0, parts, pass_on, 0)

    def close(t, _):
        buf = rows(t * part, part)
        here = ob.at[0, buf, :]
        for n in (0, 3, 4, 5, 6):
            await_bytes(here, o_recv.at[n, t])
        for n in range(8):
            await_bytes(here, o_send.at[n, t])
        for n in range(3):
            await_bytes(ybuf.at[0, buf, :], y_send.at[n, t])
            await_bytes(xbuf.at[0, buf, :], x_send.at[n, t])
        return 0

    lax.fori_loop(0, parts, close, 0)
    for n in range(3):
        await_bytes(sm.at[0], s_send.at[n])
    await_bytes(hb.at[0], h_send.at[2])
    for n in range(2):
        await_bytes(hb.at[0, across, :], h_send.at[n])
        await_bytes(hb.at[0, across, :], hf_send.at[n])

    def drain(j, _):
        for d in range(4):
            await_bytes(group(j), f_send.at[j, d])
            if d:
                await_bytes(group(j), w_send.at[j, d - 1])
        return 0

    lax.fori_loop(0, local_e, drain, 0)


def solution(mesh):
    emb_size = mesh.shape["emb"]
    ffn_size = mesh.shape["ffn"]
    assert emb_size == 4 and ffn_size == 2

    def local_block(hidden, norm_pre, norm_post, w_router, w_gate, w_up, w_down, choice):
        num_tok, lw = hidden.shape
        experts, _, fw = w_gate.shape
        top_k = choice.shape[1]
        capacity = 2 * num_tok * top_k // experts
        width, ffn = lw * emb_size, fw * ffn_size
        half, quarter, local_e = num_tok // 2, num_tok // 8, experts // 4
        small_rows = experts + 16
        row = lax.broadcasted_iota(jnp.int32, (small_rows, lw), 0)
        norms = jnp.where(row == experts, norm_pre[None, :], norm_post[None, :])
        small = jnp.where(row < experts, jnp.pad(w_router.T, ((0, 16), (0, 0))), norms)
        parts, cut = 2, 384
        bf16, f32 = jnp.bfloat16, jnp.float32
        dma = pltpu.SemaphoreType.DMA
        anywhere = pl.BlockSpec(memory_space=pl.ANY)
        flops = 2 * 3 * half * local_e * width * ffn
        return pl.pallas_call(
            functools.partial(kernel, experts, capacity),
            out_shape=jax.ShapeDtypeStruct((num_tok, lw), bf16),
            in_specs=[anywhere] * 5 + [pl.BlockSpec(memory_space=pltpu.VMEM)],
            out_specs=anywhere,
            scratch_shapes=[
                pltpu.VMEM((4, half, lw), bf16),
                pltpu.VMEM((4, small_rows, lw), bf16),
                pltpu.VMEM((local_e, 2, width, fw), bf16),
                pltpu.VMEM((local_e, 2, width, fw), bf16),
                pltpu.VMEM((local_e, 4, ffn, lw), bf16),
                pltpu.VMEM((half, width), bf16),
                pltpu.VMEM((half, experts), f32),
                pltpu.VMEM((half, width), f32),
                pltpu.VMEM((3, quarter, cut), f32),
                pltpu.VMEM((3, quarter, width - cut), f32),
                pltpu.VMEM((4, quarter, lw), bf16),
                pltpu.VMEM((quarter, ffn), bf16),
                dma((3,)), dma((4,)), dma((2,)), dma((2,)), dma((3,)), dma((4,)),
                dma((local_e, 3)), dma((local_e, 3)), dma((local_e,)),
                dma((local_e, 4)), dma((local_e, 4)),
                dma((3, parts)), dma((3, parts)), dma((3, parts)), dma((3, parts)),
                dma((8, parts)), dma((7, parts)),
            ],
            compiler_params=pltpu.CompilerParams(
                collective_id=0, has_side_effects=True, vmem_limit_bytes=67043328
            ),
            cost_estimate=pl.CostEstimate(flops=flops, bytes_accessed=60 << 20, transcendentals=half * local_e * ffn),
        )(hidden, w_gate, w_up, w_down, small, choice.T)

    in_specs = (P('dp', 'emb'), P('emb'), P('emb'), P('emb', None), P(None, 'emb', 'ffn'), P(None, 'emb', 'ffn'), P(None, 'ffn', 'emb'), P('dp', None))
    return jax.shard_map(local_block, mesh=mesh, in_specs=in_specs, out_specs=P('dp', 'emb'), check_vma=False)
```

time: 324 us -> 271 us (0.84)
  Pallas kernels: 314 us -> 266 us
  local copies, waits for them, and re-layouts: 7.27 us -> 3.05 us
    pallas_call x1, Pallas kernels: 314 us -> 266 us  [local_block(): pl.pallas_call(functools.partial(kernel, experts, capacity), out_shape=ja...]
where the time goes in v2:
time: 271 us; the launch traced here: 270 us
  Pallas kernels  266 us (98%)
  local copies, waits for them, and re-layouts  3.05 us (1%)
    pallas_call x1, Pallas kernels, local_block(): pl.pallas_call(functools.partial(kernel, experts, capacity), out_shape=ja...  266 us

profile of v2, /device:TPU:0, one launch (start us, length us, event | category | flops | bytes accessed | tf_op | source)
XLA Modules:
  0.0 270.3 jit_solution(5728637246585016290)
XLA Ops:
  0.0 1.4 select_select_fusion.small_ref
  1.4 265.8 %shard_map.82 = bf16[4096,256]{1,0:T(8,128)(2,1)} custom-call(bf16[4096,256]{1,0:T(8,128)(2,1)} %h_ref.1, bf16[32,256,256]{2,1,0:T(8,128)(2,1)} %wg_ref.1, bf16[32,256,256]{2,1,0:T(8,128)(2,1)} %wu_ref.1, bf16[32,256,256]{2,1,0:T(8,128)(2,1)} %wd_ref.1, bf16[48,256]{1,0:T(8,128)(2,1)} %select_select_fusion.small_ref, s32[8,4096]{1,0:T(8,128)} %bitcast.3), custom_call_target="tpu_custom_call" | custom-call | flops 51539607552 | bytes 62914560 | tf_op jit(solution)/shard_map/pallas_call | solution.py:353
  267.2 3.0 %copy.10 = bf16[4096,256]{1,0:T(8,128)(2,1)} copy(bf16[4096,256]{1,0:T(8,128)(2,1)} %shard_map.82) | data formatting | bytes 4194304
  (1 shorter events, 0.0 us)

commit v3 on v2

--- a/solution.py
+++ b/solution.py
@@ -13,6 +13,30 @@
 MESH = pl.DeviceIdType.MESH
 
 
+PIECES = 8
+Y_FIRST = (0, 2, 6)
+ORDER = (
+    "D3", "D1", "D2", "N2", "D4", "N5", "D6", "m2", "m3", "M2", "M3", "m1",
+    "D5", "M1", "m4", "m6", "N3", "M4", "N1", "N6", "t2", "D0", "m5", "M6",
+    "M5", "t3", "N0", "N4", "m0", "t1", "e2", "D7", "t5", "t6", "e3", "t4",
+    "e1", "M0", "N7", "m7", "M7", "e4", "e5", "e6", "t0", "t7", "e0", "e7",
+)
+
+
+def plan():
+    steps = [(p[0], int(p[1:])) for p in ORDER]
+    head = next(n for n, p in enumerate(steps) if p[0] == "m")
+    first, tile = [], 0
+    for kind, t in steps[:head]:
+        need = t // (PIECES // 2) + (2 if kind == "N" and t not in Y_FIRST else 0)
+        tile = max(tile, need)
+        first.append((kind, t, tile))
+    return first, steps[head:]
+
+
+FIRST, REST = plan()
+
+
 def gelu_tanh(z):
     return z * (0.5 * (1.0 + jnp.tanh(math.sqrt(2.0 / math.pi) * (z + 0.044715 * (z * z * z)))))
 
@@ -20,9 +44,9 @@
 def kernel(
     experts, capacity,
     h_ref, wg_ref, wu_ref, wd_ref, small_ref, choice_ref, out_ref,
-    hb, sm, w0, w1, w2, xn, gates, acc, ybuf, xbuf, ob, gb,
+    hb, sm, w0, w1, w2, xn, gates, acc, rbuf, sq_own, sq_far, ob, gb,
     h_send, h_recv, hf_send, hf_recv, s_send, s_recv, w_send, w_recv, w_own, f_send, f_recv,
-    y_send, y_recv, x_send, x_recv, o_send, o_recv,
+    r_send, r_recv, q_send, q_recv, o_send, o_recv,
 ):
     num_tok, lw = h_ref.shape
     fw = wg_ref.shape[2]
@@ -30,9 +54,8 @@
     quarter = num_tok // 8
     local_e = experts // 4
     tile = 256
-    parts = y_recv.shape[1]
-    part = quarter // parts
-    cut = ybuf.shape[2]
+    part = 128
+    parts = quarter * 2 // part
     bf16, f32 = jnp.bfloat16, jnp.float32
 
     f = lax.axis_index("ffn")
@@ -103,7 +126,7 @@
             for src, to in zip((wg_ref.at[e2], wu_ref.at[e2], wd_ref.at[e2]), dst):
                 remote(src, to, w_send.at[j, d - 1], w_recv.at[j, d - 1], f2, 2 * x2 + c).start()
 
-    ahead = 4
+    ahead = 3
     for j in range(2):
         send_expert(j)
 
@@ -127,7 +150,8 @@
         a = chosen(c * half + n * tile)
         before = carry + jnp.dot(a.astype(bf16), strict, preferred_element_type=f32)
         gates[rows(n * tile, tile), :] = jnp.where(before < capacity, a, 0.0).T
-        acc[rows(n * tile, tile), :] = jnp.zeros((tile, acc.shape[1]), f32)
+        for xs in range(2):
+            acc[xs, rows(n * tile, tile), :] = jnp.zeros((tile, 2 * lw), f32)
         return carry + jnp.sum(a, axis=1, keepdims=True)
 
     lax.fori_loop(0, half // tile, place, first * c.astype(f32))
@@ -166,33 +190,25 @@
 
     lax.fori_loop(0, half // tile, route, 0)
 
-    def to_y(src, slot, t):
-        return remote(
-            src, ybuf.at[slot, rows(t * part, part), :], y_send.at[slot, t], y_recv.at[slot, t], 1 - f, i
-        )
-
-    def to_x(src, slot, t):
-        return remote(
-            src, xbuf.at[slot, rows(t * part, part), :], x_send.at[slot, t], x_recv.at[slot, t], f, 2 * (1 - x) + c
-        )
-
-    def y_to_x(src, t):
-        return remote(
-            src, ybuf.at[2, rows(t * part, part), :], y_send.at[2, t], y_recv.at[2, t], f, 2 * (1 - x) + c
-        )
-
-    def x_to_y(src, t):
-        return remote(src, xbuf.at[2, rows(t * part, part), :], x_send.at[2, t], x_recv.at[2, t], 1 - f, i)
-
-    def out_rows(xs, fs, cs, t):
-        return rows(cs * half + (2 * xs + fs) * quarter + t * part, part)
+    def piece(xs, fs, t):
+        return acc.at[xs, rows(fs * 2 * quarter + t * part, part), :]
+
+    def landing(slot, t):
+        return rbuf.at[slot, rows(t * part, part), :]
+
+    def along_x(src, slot, t):
+        return remote(src, landing(slot, t), r_send.at[slot, t], r_recv.at[slot, t], f, 2 * (1 - x) + c)
+
+    def along_y(src, slot, t):
+        return remote(src, landing(slot, t), r_send.at[slot, t], r_recv.at[slot, t], 1 - f, i)
 
     lane_q = lax.broadcasted_iota(jnp.int32, (quarter, experts), 1)
 
-    def expert(j, _):
-        @pl.when(j + ahead < local_e)
-        def _():
-            send_expert(j + ahead)
+    def expert(j, last):
+        if not last:
+            @pl.when(j + ahead < local_e)
+            def _():
+                send_expert(j + ahead)
 
         await_bytes(group(j), w_own.at[j])
         for d in (1, 2, 3):
@@ -204,9 +220,7 @@
             await_bytes(group(j), f_recv.at[j, d])
 
         def step(n, _):
-            x2 = (x + n + 1) % 2
-            f2 = (f + 1 - n // 2) % 2
-            r = rows((2 * x2 + f2) * quarter, quarter)
+            r = rows((((1 - f) * 2 + n) % 4) * quarter, quarter)
             gate = jnp.sum(jnp.where(lane_q == local_e * q + j, gates[r, :], 0.0), axis=1, keepdims=True)
             for s in range(2):
                 z0 = jnp.dot(xn[r, :], w0[j, s], preferred_element_type=f32).astype(bf16).astype(f32)
@@ -216,102 +230,101 @@
             for b in range(4):
                 y = jnp.dot(gb[...], w2[j, b], preferred_element_type=f32).astype(bf16).astype(f32)
                 u = (y * gate).astype(bf16).astype(f32)
-                acc[r, b * lw : (b + 1) * lw] += u
-
-            start = (2 * x2 + f2) * quarter
-
-            @pl.when((j == local_e - 1) & (n < 2))
-            def _():
-                for t in range(parts):
-                    src = acc.at[rows(start + t * part, part), 0:cut]
-                    to_y(src, n, t).start()
-
-            @pl.when((j == local_e - 1) & (n % 2 == 0) & (n < 3))
-            def _():
-                for t in range(parts):
-                    src = acc.at[rows(start + t * part, part), cut:]
-                    to_x(src, n // 2, t).start()
+                acc[b // 2, r, (b % 2) * lw : (b % 2 + 1) * lw] += u
+
+            if last:
+                for k in range(4):
+                    starts = [p for p in FIRST if p[2] == k]
+                    if starts:
+                        @pl.when(n == k)
+                        def _():
+                            for kind, t, _k in starts:
+                                start_piece(kind, t)
 
             return 0
 
         lax.fori_loop(0, 4, step, 0)
+
+    def start_piece(kind, t):
+        along_first, along_last = (along_y, along_x) if t in Y_FIRST else (along_x, along_y)
+        near = (x, 1 - f) if t in Y_FIRST else (1 - x, f)
+        if kind == "D":
+            along_first(piece(1 - x, 1 - f, t), 0, t).start()
+        elif kind == "N":
+            along_first(piece(*near, t), 1, t).start()
+        else:
+            far = (1 - x, f) if t in Y_FIRST else (x, 1 - f)
+            along_last(piece(*far, t), 2, t).start()
+
+    def experts_but_last(j, _):
+        expert(j, False)
         return 0
 
-    lax.fori_loop(0, local_e, expert, 0)
-
-    def mid(t, _):
-        xr = rows((2 * (1 - x) + f) * quarter + t * part, part)
-        yr = rows((2 * x + 1 - f) * quarter + t * part, part)
-        buf = rows(t * part, part)
-        await_bytes(xbuf.at[0, buf, :], x_recv.at[0, t])
-        acc[yr, cut:] = acc[yr, cut:] + xbuf[0, buf, :]
-        x_to_y(acc.at[yr, cut:], t).start()
-        await_bytes(ybuf.at[0, buf, :], y_recv.at[0, t])
-        acc[xr, 0:cut] = acc[xr, 0:cut] + ybuf[0, buf, :]
-        y_to_x(acc.at[xr, 0:cut], t).start()
+    lax.fori_loop(0, local_e - 1, experts_but_last, 0)
+    expert(local_e - 1, True)
+
+    def add_to(xs, fs, t):
+        r = rows(fs * 2 * quarter + t * part, part)
+        await_bytes(landing(0, t), r_recv.at[0, t])
+        acc[xs, r, :] = acc[xs, r, :] + rbuf[0, rows(t * part, part), :]
+
+    def total(t):
+        r = rows(f * 2 * quarter + t * part, part)
+        s = rows(t * part, part)
+        for slot in (1, 2):
+            await_bytes(landing(slot, t), r_recv.at[slot, t])
+        v = acc[x, r, :] + (rbuf[1, s, :] + rbuf[2, s, :])
+        acc[x, r, :] = v
+        v = v * v
+        v = (v[:, 0:128] + v[:, 128:256]) + (v[:, 256:384] + v[:, 384:512])
+        sq_own[t] = jnp.broadcast_to(jnp.sum(v.T, axis=0, keepdims=True), (8, part))
+        remote(sq_own.at[t], sq_far.at[t], q_send.at[t], q_recv.at[t], f, 2 * (1 - x) + c).start()
+
+    def out_rows(fs, cs, t):
+        return out_ref.at[rows(cs * half + fs * 2 * quarter + t * part, part), :]
+
+    def emit(t):
+        r = rows(f * 2 * quarter + t * part, part)
+        s = rows(t * part, part)
+        await_bytes(sq_far.at[t], q_recv.at[t])
+        inv = lax.rsqrt((sq_own[t, 0:1, :] + sq_far[t, 0:1, :]) / (4 * lw) + EPS)
+        inv = jnp.broadcast_to(inv, (part, part)).T
+        for b in range(2):
+            post = sm[2 * x + b, experts + 1 : experts + 2, :].astype(f32)
+            for g in range(lw // part):
+                cols = slice(g * part, (g + 1) * part)
+                m = acc[x, r, b * lw + g * part : b * lw + (g + 1) * part]
+                hv = hb[2 * x + b, r, cols].astype(f32)
+                ob[b, s, cols] = (hv + m * inv * post[:, cols]).astype(bf16)
+        for b in range(2):
+            remote(
+                ob.at[b, s, :], out_rows(f, c, t), o_send.at[b, t], o_recv.at[c, t], 1 - f, 2 * x + b
+            ).start()
+        pltpu.make_async_copy(ob.at[c, s, :], out_rows(f, c, t), o_send.at[2, t]).start()
+        remote(ob.at[1 - c, s, :], out_rows(f, c, t), o_send.at[3, t], o_recv.at[2, t], f, sib).start()
+
+    for kind, t in REST:
+        if kind == "m":
+            add_to(*((1 - x, f) if t in Y_FIRST else (x, 1 - f)), t)
+        elif kind == "t":
+            total(t)
+        elif kind == "e":
+            emit(t)
+        else:
+            start_piece(kind, t)
+
+    def close(t, _):
+        here = ob.at[0, rows(t * part, part), :]
+        for n in range(3):
+            await_bytes(here, o_recv.at[n, t])
+            await_bytes(landing(0, t), r_send.at[n, t])
+        for n in range(4):
+            await_bytes(here, o_send.at[n, t])
+        await_bytes(sq_own.at[t], q_send.at[t])
         return 0
 
-    lax.fori_loop(0, parts, mid, 0)
-
-    step_rows = 128
-
-    def finish(t, _):
-        buf = rows(t * part, part)
-        for n in (1, 2):
-            await_bytes(ybuf.at[n, buf, :], y_recv.at[n, t])
-            await_bytes(xbuf.at[n, buf, :], x_recv.at[n, t])
-
-        def norm(n, _):
-            r = rows(q * quarter + t * part + n * step_rows, step_rows)
-            s = rows(t * part + n * step_rows, step_rows)
-            lo = acc[r, 0:cut] + (ybuf[1, s, :] + ybuf[2, s, :])
-            hi = acc[r, cut:] + (xbuf[1, s, :] + xbuf[2, s, :])
-            sq = jnp.sum(lo * lo, axis=1, keepdims=True) + jnp.sum(hi * hi, axis=1, keepdims=True)
-            inv = lax.rsqrt(sq / (4 * lw) + EPS)
-            acc[r, 0:cut] = lo * inv
-            acc[r, cut:] = hi * inv
-            for b in range(4):
-                post = sm[b, experts + 1 : experts + 2, :].astype(f32)
-                ob[b, s, :] = (hb[b, r, :].astype(f32) + acc[r, b * lw : (b + 1) * lw] * post).astype(bf16)
-            return 0
-
-        lax.fori_loop(0, part // step_rows, norm, 0)
-
-        mine = out_ref.at[out_rows(x, f, c, t), :]
-        for c2 in range(2):
-            i2 = 2 * (1 - x) + c2
-            remote(ob.at[i2, buf, :], mine, o_send.at[2 + c2, t], o_recv.at[1 + c, t], f, i2).start()
-        for c2 in range(2):
-            i2 = 2 * x + c2
-            remote(ob.at[i2, buf, :], mine, o_send.at[4 + c2, t], o_recv.at[3 + c, t], 1 - f, i2).start()
-        pltpu.make_async_copy(ob.at[i, buf, :], mine, o_send.at[0, t]).start()
-        remote(ob.at[sib, buf, :], mine, o_send.at[1, t], o_recv.at[0, t], f, sib).start()
-        return 0
-
-    lax.fori_loop(0, parts, finish, 0)
-
-    def pass_on(t, _):
-        for c2 in range(2):
-            there = out_ref.at[out_rows(1 - x, f, c2, t), :]
-            await_bytes(there, o_recv.at[1 + c2, t])
-            remote(there, there, o_send.at[6 + c2, t], o_recv.at[5 + c2, t], 1 - f, i).start()
-        return 0
-
-    lax.fori_loop(0, parts, pass_on, 0)
-
-    def close(t, _):
-        buf = rows(t * part, part)
-        here = ob.at[0, buf, :]
-        for n in (0, 3, 4, 5, 6):
-            await_bytes(here, o_recv.at[n, t])
-        for n in range(8):
-            await_bytes(here, o_send.at[n, t])
-        for n in range(3):
-            await_bytes(ybuf.at[0, buf, :], y_send.at[n, t])
-            await_bytes(xbuf.at[0, buf, :], x_send.at[n, t])
-        return 0
-
     lax.fori_loop(0, parts, close, 0)
+
     for n in range(3):
         await_bytes(sm.at[0], s_send.at[n])
     await_bytes(hb.at[0], h_send.at[2])
@@ -345,7 +358,7 @@
         row = lax.broadcasted_iota(jnp.int32, (small_rows, lw), 0)
         norms = jnp.where(row == experts, norm_pre[None, :], norm_post[None, :])
         small = jnp.where(row < experts, jnp.pad(w_router.T, ((0, 16), (0, 0))), norms)
-        parts, cut = 2, 384
+        parts = 2 * quarter // 128
         bf16, f32 = jnp.bfloat16, jnp.float32
         dma = pltpu.SemaphoreType.DMA
         anywhere = pl.BlockSpec(memory_space=pl.ANY)
@@ -363,16 +376,17 @@
                 pltpu.VMEM((local_e, 4, ffn, lw), bf16),
                 pltpu.VMEM((half, width), bf16),
                 pltpu.VMEM((half, experts), f32),
-                pltpu.VMEM((half, width), f32),
-                pltpu.VMEM((3, quarter, cut), f32),
-                pltpu.VMEM((3, quarter, width - cut), f32),
-                pltpu.VMEM((4, quarter, lw), bf16),
+                pltpu.VMEM((2, half, width // 2), f32),
+                pltpu.VMEM((3, 2 * quarter, width // 2), f32),
+                pltpu.VMEM((parts, 8, 128), f32),
+                pltpu.VMEM((parts, 8, 128), f32),
+                pltpu.VMEM((2, 2 * quarter, lw), bf16),
                 pltpu.VMEM((quarter, ffn), bf16),
                 dma((3,)), dma((4,)), dma((2,)), dma((2,)), dma((3,)), dma((4,)),
                 dma((local_e, 3)), dma((local_e, 3)), dma((local_e,)),
                 dma((local_e, 4)), dma((local_e, 4)),
-                dma((3, parts)), dma((3, parts)), dma((3, parts)), dma((3, parts)),
-                dma((8, parts)), dma((7, parts)),
+                dma((3, parts)), dma((3, parts)), dma((parts,)), dma((parts,)),
+                dma((4, parts)), dma((3, parts)),
             ],
             compiler_params=pltpu.CompilerParams(
                 collective_id=0, has_side_effects=True, vmem_limit_bytes=67043328

time: 271 us -> 262 us (0.967)
  Pallas kernels: 266 us -> 257 us
    pallas_call x1, Pallas kernels: 266 us -> 257 us  [local_block(): pl.pallas_call(functools.partial(kernel, experts, capacity), out_shape=ja...]
where the time goes in v3:
time: 262 us; the launch traced here: 261 us
  Pallas kernels  257 us (98%)
  local copies, waits for them, and re-layouts  3.05 us (1%)
    pallas_call x1, Pallas kernels, local_block(): pl.pallas_call(functools.partial(kernel, experts, capacity), out_shape=ja...  257 us

profile of v3, /device:TPU:0, one launch (start us, length us, event | category | flops | bytes accessed | tf_op | source)
XLA Modules:
  0.0 261.4 jit_solution(7587481900286513910)
XLA Ops:
  0.0 1.4 select_select_fusion.small_ref
  1.4 256.9 %shard_map.82 = bf16[4096,256]{1,0:T(8,128)(2,1)} custom-call(bf16[4096,256]{1,0:T(8,128)(2,1)} %h_ref.1, bf16[32,256,256]{2,1,0:T(8,128)(2,1)} %wg_ref.1, bf16[32,256,256]{2,1,0:T(8,128)(2,1)} %wu_ref.1, bf16[32,256,256]{2,1,0:T(8,128)(2,1)} %wd_ref.1, bf16[48,256]{1,0:T(8,128)(2,1)} %select_select_fusion.small_ref, s32[8,4096]{1,0:T(8,128)} %bitcast.3), custom_call_target="tpu_custom_call" | custom-call | flops 51539607552 | bytes 62914560 | tf_op jit(solution)/shard_map/pallas_call | solution.py:366
  258.3 3.0 %copy.10 = bf16[4096,256]{1,0:T(8,128)(2,1)} copy(bf16[4096,256]{1,0:T(8,128)(2,1)} %shard_map.82) | data formatting | bytes 4194304
  (1 shorter events, 0.0 us)

commit v4 on v3

v4 whole, which is shorter than its diff:
```python
import functools
import math

import jax
import jax.numpy as jnp
from jax import lax
from jax.experimental import pallas as pl
from jax.experimental.pallas import tpu as pltpu
from jax.sharding import PartitionSpec as P

EPS = 1e-5
LANES = 128
MESH = pl.DeviceIdType.MESH


PIECES = 16
Y_FIRST = (2, 6, 8, 10, 13)
ORDER = (
    "D3", "D0", "D1", "D2", "N2", "N6", "D5", "N13", "N5", "D6", "m2", "m3", "m0", "D7", "N10", "m1",
    "N0", "M3", "m5", "D4", "D10", "m6", "M6", "M1", "m7", "N1", "M0", "N11", "D13", "m4", "m10", "N3",
    "M4", "M2", "D8", "t0", "M7", "m13", "N4", "N8", "D12", "M5", "D9", "m8", "t1", "e0", "M8", "m12",
    "M12", "N9", "N7", "t2", "m9", "M9", "e1", "D11", "M10", "D15", "t4", "t3", "e2", "m11", "M11", "N12",
    "M13", "D14", "m15", "M15", "e3", "t5", "e4", "N14", "t6", "N15", "m14", "M14", "e5", "e6", "t7", "e7",
)


def plan():
    steps = [(p[0], int(p[1:])) for p in ORDER]
    head = next(n for n, p in enumerate(steps) if p[0] == "m")
    first, tile = [], 0
    for kind, t in steps[:head]:
        need = t // 4 + (4 if kind == "N" and t not in Y_FIRST else 0)
        tile = max(tile, need)
        first.append((kind, t, tile))
    return first, steps[head:]


FIRST, REST = plan()


def gelu_tanh(z):
    return z * (0.5 * (1.0 + jnp.tanh(math.sqrt(2.0 / math.pi) * (z + 0.044715 * (z * z * z)))))


def kernel(
    experts, capacity,
    h_ref, wg_ref, wu_ref, wd_ref, wr_ref, pre_ref, post_ref, choice_hbm, out_ref,
    choice_ref, hb, wr, pre, post, w0, w1, w2, xn, gates, acc, rbuf, sq_own, sq_far, ob, gb,
    h_send, h_recv, hf_send, hf_recv, s_send, s_recv, n_send, n_recv, c_sem, w_send, w_recv, w_own, f_send, f_recv,
    r_send, r_recv, q_send, q_recv, o_send, o_recv,
):
    num_tok, lw = h_ref.shape
    fw = wg_ref.shape[2]
    half = num_tok // 2
    quarter = num_tok // 8
    local_e = experts // 4
    tile = 256
    part = 128
    parts = quarter * 2 // part
    bf16, f32 = jnp.bfloat16, jnp.float32

    f = lax.axis_index("ffn")
    i = lax.axis_index("emb")
    x, c = i // 2, i % 2
    q = 2 * x + f
    sib = 2 * x + (1 - c)

    def chip(d):
        x2 = (x + d // 2) % 2
        f2 = (f + d % 2) % 2
        return x2, f2, 2 * x2 + f2

    def rows(start, size):
        return pl.ds(pl.multiple_of(start, 128), size)

    pltpu.make_async_copy(choice_hbm, choice_ref, c_sem).start()

    barrier = pltpu.get_barrier_semaphore()
    for df in range(2):
        for di in range(4):
            if df or di:
                pl.semaphore_signal(
                    barrier, inc=1, device_id={"ffn": (f + df) % 2, "emb": (i + di) % 4}, device_id_type=MESH
                )
    pl.semaphore_wait(barrier, 7)

    def remote(src, dst, send, recv, f2, i2):
        return pltpu.make_async_remote_copy(
            src_ref=src, dst_ref=dst, send_sem=send, recv_sem=recv,
            device_id={"ffn": f2, "emb": i2}, device_id_type=MESH,
        )

    def await_bytes(ref, sem):
        pltpu.make_async_copy(ref, ref, sem).wait()

    cols = pl.ds(pl.multiple_of(i * lw, 256), lw)

    def send_small(i2):
        remote(wr_ref, wr.at[i], s_send, s_recv.at[i], f, i2).start()
        remote(pre_ref, pre.at[cols], n_send.at[0], n_recv.at[0, i], f, i2).start()
        remote(post_ref, post.at[cols], n_send.at[1], n_recv.at[1, i], f, i2).start()

    own_h = pltpu.make_async_copy(h_ref.at[rows(c * half, half), :], hb.at[i], h_recv.at[i])
    own_h.start()
    pltpu.make_async_copy(wr_ref, wr.at[i], s_recv.at[i]).start()
    pltpu.make_async_copy(pre_ref, pre.at[cols], n_recv.at[0, i]).start()
    pltpu.make_async_copy(post_ref, post.at[cols], n_recv.at[1, i]).start()
    across = rows(f * (half // 2), half // 2)
    far = rows((1 - f) * (half // 2), half // 2)
    for c2 in range(2):
        i2 = 2 * (1 - x) + c2
        send_small(i2)
        src = h_ref.at[rows(c2 * half + f * (half // 2), half // 2), :]
        remote(src, hb.at[i, across, :], h_send.at[c2], h_recv.at[i], f, i2).start()
    send_small(sib)
    remote(h_ref.at[rows((1 - c) * half, half), :], hb.at[i], h_send.at[2], h_recv.at[i], f, sib).start()

    def blocks(j, fs, es):
        return (
            w0.at[j, fs, rows(es * lw, lw), :],
            w1.at[j, fs, rows(es * lw, lw), :],
            w2.at[j, es, rows(fs * fw, fw), :],
        )

    def group(j):
        return w0.at[j, 0, pl.ds(0, 3 * lw), :]

    def send_expert(j):
        dst = blocks(j, f, i)
        e = local_e * q + j
        for src, to in zip((wg_ref.at[e], wu_ref.at[e], wd_ref.at[e]), dst):
            pltpu.make_async_copy(src, to, w_own.at[j]).start()
            remote(src, to, f_send.at[0], f_recv.at[j, 0], f, sib).start()
        for m in range(3):
            for d in (3 - c, 2 + c, 1):
                x2, f2, q2 = chip(d)
                e2 = local_e * q2 + j
                src = (wg_ref.at[e2], wu_ref.at[e2], wd_ref.at[e2])[m]
                remote(src, dst[m], w_send.at[d - 1], w_recv.at[j, d - 1], f2, 2 * x2 + c).start()

    ahead = 3
    for j in range(2):
        send_expert(j)

    await_bytes(choice_ref, c_sem)

    sublane = lax.broadcasted_iota(jnp.int32, (experts, tile), 0)

    def chosen(start):
        ch = choice_ref[:, pl.ds(pl.multiple_of(start, LANES), tile)]
        a = jnp.zeros((experts, tile), f32)
        for k in range(choice_ref.shape[0]):
            a = a + jnp.where(ch[k : k + 1, :] == sublane, 1.0, 0.0)
        return a

    def count(n, total):
        return total + jnp.sum(chosen(n * tile), axis=1, keepdims=True)

    first = lax.fori_loop(0, half // tile, count, jnp.zeros((experts, 1), f32))
    strict = lax.broadcasted_iota(jnp.int32, (tile, tile), 0) < lax.broadcasted_iota(jnp.int32, (tile, tile), 1)
    strict = jnp.where(strict, 1.0, 0.0).astype(bf16)

    def place(n, carry):
        a = chosen(c * half + n * tile)
        before = carry + jnp.dot(a.astype(bf16), strict, preferred_element_type=f32)
        gates[rows(n * tile, tile), :] = jnp.where(before < capacity, a, 0.0).T
        for b in range(4):
            acc[b, rows(n * tile, tile), :] = jnp.zeros((tile, lw), f32)
        return carry + jnp.sum(a, axis=1, keepdims=True)

    lax.fori_loop(0, half // tile, place, first * c.astype(f32))

    for c2 in range(2):
        e2 = 2 * (1 - x) + c2
        await_bytes(hb.at[e2, across, :], h_recv.at[e2])
        ref = hb.at[e2, across, :]
        remote(ref, ref, hf_send.at[c2], hf_recv.at[c2], 1 - f, i).start()
    for j in range(2, ahead):
        send_expert(j)
    for c2 in range(2):
        await_bytes(hb.at[2 * x + c2], h_recv.at[2 * x + c2])
        await_bytes(hb.at[2 * (1 - x) + c2, far, :], hf_recv.at[c2])
    for b in range(4):
        await_bytes(wr.at[b], s_recv.at[b])
        for n, ref in enumerate((pre, post)):
            await_bytes(ref.at[pl.ds(b * lw, lw)], n_recv.at[n, b])

    def route(n, _):
        r = rows(n * tile, tile)
        sq = jnp.zeros((tile, 1), f32)
        for b in range(4):
            hv = hb[b, r, :].astype(f32)
            sq = sq + jnp.sum(hv * hv, axis=1, keepdims=True)
        inv = lax.rsqrt(sq / (4 * lw) + EPS)
        logits = jnp.zeros((tile, experts), f32)
        for b in range(4):
            normed = (hb[b, r, :].astype(f32) * inv * pre[b * lw : (b + 1) * lw].astype(f32)[None, :]).astype(bf16)
            xn[r, b * lw : (b + 1) * lw] = normed
            logits = logits + lax.dot_general(
                normed, wr[b], (((1,), (1,)), ((), ())), preferred_element_type=f32
            )
        p = jnp.exp(logits - jnp.max(logits, axis=1, keepdims=True))
        p = p / jnp.sum(p, axis=1, keepdims=True)
        gates[r, :] = jnp.where(gates[r, :] > 0.0, p, 0.0)
        return 0

    lax.fori_loop(0, half // tile, route, 0)

    def piece(xs, fs, t):
        return acc.at[2 * xs + t % 2, rows(fs * 2 * quarter + t // 2 * part, part), :]

    def landing(slot, t):
        return rbuf.at[slot, t % 2, rows(t // 2 * part, part), :]

    def along_x(src, slot, t):
        return remote(src, landing(slot, t), r_send.at[slot], r_recv.at[slot, t], f, 2 * (1 - x) + c)

    def along_y(src, slot, t):
        return remote(src, landing(slot, t), r_send.at[slot], r_recv.at[slot, t], 1 - f, i)

    lane_q = lax.broadcasted_iota(jnp.int32, (quarter, experts), 1)

    def expert(j, last):
        if not last:
            @pl.when(j + ahead < local_e)
            def _():
                send_expert(j + ahead)

        await_bytes(group(j), w_own.at[j])
        for d in (1, 2, 3):
            x2, f2, _q2 = chip(d)
            await_bytes(group(j), w_recv.at[j, d - 1])
            for ref in blocks(j, f2, 2 * x2 + c):
                remote(ref, ref, f_send.at[d], f_recv.at[j, d], f, sib).start()
        for d in range(4):
            await_bytes(group(j), f_recv.at[j, d])

        count = 8 if last else 4
        size = half // count

        def step(n, _):
            r = rows((((1 - f) * count // 2 + n) % count) * size, size)
            gate = jnp.sum(jnp.where(lane_q[0:size] == local_e * q + j, gates[r, :], 0.0), axis=1, keepdims=True)
            for s in range(2):
                z0 = jnp.dot(xn[r, :], w0[j, s], preferred_element_type=f32).astype(bf16).astype(f32)
                z1 = jnp.dot(xn[r, :], w1[j, s], preferred_element_type=f32).astype(bf16).astype(f32)
                g = jnp.where(gate > 0.0, gelu_tanh(z0) * z1, 0.0)
                gb[0:size, s * fw : (s + 1) * fw] = g.astype(bf16)
            for b in range(4):
                y = jnp.dot(gb[0:size, :], w2[j, b], preferred_element_type=f32).astype(bf16).astype(f32)
                u = (y * gate).astype(bf16).astype(f32)
                acc[b, r, :] += u

            if last:
                for k in range(count):
                    starts = [p for p in FIRST if p[2] == k]
                    if starts:
                        @pl.when(n == k)
                        def _():
                            for kind, t, _k in starts:
                                start_piece(kind, t)

            return 0

        lax.fori_loop(0, count, step, 0)

    def start_piece(kind, t):
        along_first, along_last = (along_y, along_x) if t in Y_FIRST else (along_x, along_y)
        near = (x, 1 - f) if t in Y_FIRST else (1 - x, f)
        if kind == "D":
            along_first(piece(1 - x, 1 - f, t), 0, t).start()
        elif kind == "N":
            along_first(piece(*near, t), 1, t).start()
        else:
            far = (1 - x, f) if t in Y_FIRST else (x, 1 - f)
            along_last(piece(*far, t), 2, t).start()

    def experts_but_last(j, _):
        expert(j, False)
        return 0

    lax.fori_loop(0, local_e - 1, experts_but_last, 0)
    expert(local_e - 1, True)

    def add_to(xs, fs, t):
        here = piece(xs, fs, t)
        await_bytes(landing(0, t), r_recv.at[0, t])
        here[...] = here[...] + landing(0, t)[...]

    def total(t):
        r = rows(f * 2 * quarter + t * part, part)
        s = rows(t * part, part)
        sq = jnp.zeros((part, part), f32)
        for b in range(2):
            for slot in (1, 2):
                await_bytes(landing(slot, 2 * t + b), r_recv.at[slot, 2 * t + b])
            v = acc[2 * x + b, r, :] + (rbuf[1, b, s, :] + rbuf[2, b, s, :])
            acc[2 * x + b, r, :] = v
            v = v * v
            sq = sq + (v[:, 0:128] + v[:, 128:256])
        sq_own[t] = jnp.broadcast_to(jnp.sum(sq.T, axis=0, keepdims=True), (8, part))
        remote(sq_own.at[t], sq_far.at[t], q_send, q_recv.at[t], f, 2 * (1 - x) + c).start()

    def out_rows(fs, cs, t):
        return out_ref.at[rows(cs * half + fs * 2 * quarter + t * part, part), :]

    def emit(t):
        r = rows(f * 2 * quarter + t * part, part)
        s = rows(t * part, part)
        await_bytes(sq_far.at[t], q_recv.at[t])
        inv = lax.rsqrt((sq_own[t, 0:1, :] + sq_far[t, 0:1, :]) / (4 * lw) + EPS)
        inv = jnp.broadcast_to(inv, (part, part)).T
        for b in range(2):
            gain = post[pl.ds(pl.multiple_of((2 * x + b) * lw, 256), lw)].astype(f32)[None, :]
            for g in range(lw // part):
                cols = slice(g * part, (g + 1) * part)
                m = acc[2 * x + b, r, cols]
                hv = hb[2 * x + b, r, cols].astype(f32)
                ob[b, s, cols] = (hv + m * inv * gain[:, cols]).astype(bf16)
        for b in range(2):
            remote(
                ob.at[b, s, :], out_rows(f, c, t), o_send.at[b], o_recv.at[c, t], 1 - f, 2 * x + b
            ).start()
        own = rows(c * half + f * 2 * quarter + t * part, part)
        out_ref[own, :] = ob[c, s, :]
        remote(ob.at[1 - c, s, :], out_rows(f, c, t), o_send.at[2], o_recv.at[2, t], f, sib).start()

    for kind, t in REST:
        if kind == "m":
            add_to(*((1 - x, f) if t in Y_FIRST else (x, 1 - f)), t)
        elif kind == "t":
            total(t)
        elif kind == "e":
            emit(t)
        else:
            start_piece(kind, t)

    def close(t, _):
        here = ob.at[0, rows(t * part, part), :]
        for n in range(3):
            await_bytes(here, o_recv.at[n, t])
        return 0

    lax.fori_loop(0, parts, close, 0)
    for n in range(3):
        await_bytes(ob.at[0], o_send.at[n])
        await_bytes(rbuf.at[0], r_send.at[n])
    await_bytes(sq_own, q_send)

    await_bytes(wr.at[pl.ds(0, 3)], s_send)
    for n in range(2):
        await_bytes(pre.at[pl.ds(0, 3 * lw)], n_send.at[n])
    await_bytes(hb.at[0], h_send.at[2])
    for n in range(2):
        await_bytes(hb.at[0, across, :], h_send.at[n])
        await_bytes(hb.at[0, across, :], hf_send.at[n])

    sent = w0.at[pl.ds(0, 3 * local_e // 8)]
    for d in range(4):
        await_bytes(sent, f_send.at[d])
        if d:
            await_bytes(sent, w_send.at[d - 1])


def solution(mesh):
    emb_size = mesh.shape["emb"]
    ffn_size = mesh.shape["ffn"]
    assert emb_size == 4 and ffn_size == 2

    def local_block(hidden, norm_pre, norm_post, w_router, w_gate, w_up, w_down, choice):
        num_tok, lw = hidden.shape
        experts, _, fw = w_gate.shape
        top_k = choice.shape[1]
        capacity = 2 * num_tok * top_k // experts
        width, ffn = lw * emb_size, fw * ffn_size
        half, quarter, local_e = num_tok // 2, num_tok // 8, experts // 4
        parts = 2 * quarter // 128
        bf16, f32 = jnp.bfloat16, jnp.float32
        dma = pltpu.SemaphoreType.DMA
        anywhere = pl.BlockSpec(memory_space=pl.ANY)
        flops = 2 * 3 * half * local_e * width * ffn
        return pl.pallas_call(
            functools.partial(kernel, experts, capacity),
            out_shape=pltpu.VMEM((num_tok, lw), bf16),
            in_specs=[anywhere] * 8,
            out_specs=pl.BlockSpec(memory_space=pltpu.VMEM),
            scratch_shapes=[
                pltpu.VMEM((top_k, num_tok), jnp.int32),
                pltpu.VMEM((4, half, lw), bf16),
                pltpu.VMEM((4, experts, lw), bf16),
                pltpu.VMEM((width,), bf16),
                pltpu.VMEM((width,), bf16),
                pltpu.VMEM((local_e, 2, width, fw), bf16),
                pltpu.VMEM((local_e, 2, width, fw), bf16),
                pltpu.VMEM((local_e, 4, ffn, lw), bf16),
                pltpu.VMEM((half, width), bf16),
                pltpu.VMEM((half, experts), f32),
                pltpu.VMEM((4, half, lw), f32),
                pltpu.VMEM((3, 2, 2 * quarter, lw), f32),
                pltpu.VMEM((parts, 8, 128), f32),
                pltpu.VMEM((parts, 8, 128), f32),
                pltpu.VMEM((2, 2 * quarter, lw), bf16),
                pltpu.VMEM((quarter, ffn), bf16),
                dma((3,)), dma((4,)), dma((2,)), dma((2,)), dma(()), dma((4,)), dma((2,)), dma((2, 4)), dma(()),
                dma((3,)), dma((local_e, 3)), dma((local_e,)),
                dma((4,)), dma((local_e, 4)),
                dma((3,)), dma((3, 2 * parts)), dma(()), dma((parts,)),
                dma((3,)), dma((3, parts)),
            ],
            compiler_params=pltpu.CompilerParams(
                collective_id=0, has_side_effects=True, vmem_limit_bytes=58 << 20
            ),
            cost_estimate=pl.CostEstimate(flops=flops, bytes_accessed=60 << 20, transcendentals=half * local_e * ffn),
        )(hidden, w_gate, w_up, w_down, w_router.T, norm_pre, norm_post, choice.T)

    in_specs = (P('dp', 'emb'), P('emb'), P('emb'), P('emb', None), P(None, 'emb', 'ffn'), P(None, 'emb', 'ffn'), P(None, 'ffn', 'emb'), P('dp', None))
    return jax.shard_map(local_block, mesh=mesh, in_specs=in_specs, out_specs=P('dp', 'emb'), check_vma=False)
```

time: 262 us -> 254 us (0.969)
  Pallas kernels: 257 us -> 253 us
    pallas_call x1, Pallas kernels: 257 us -> 253 us  [local_block(): pl.pallas_call(functools.partial(kernel, experts, capacity), out_shape=pl...]
where the time goes in v4:
time: 254 us
  Pallas kernels  253 us (100%)
    pallas_call x1, Pallas kernels, local_block(): pl.pallas_call(functools.partial(kernel, experts, capacity), out_shape=pl...  253 us

profile of v4, /device:TPU:0, one launch (start us, length us, event | category | flops | bytes accessed | tf_op | source)
XLA Modules:
  0.0 253.9 jit_solution(17606750346713905974)
XLA Ops:
  0.0 252.6 %shard_map.82 = bf16[4096,256]{1,0:T(8,128)(2,1)S(1)} custom-call(bf16[4096,256]{1,0:T(8,128)(2,1)} %h_ref.1, bf16[32,256,256]{2,1,0:T(8,128)(2,1)} %wg_ref.1, bf16[32,256,256]{2,1,0:T(8,128)(2,1)} %wu_ref.1, bf16[32,256,256]{2,1,0:T(8,128)(2,1)} %wd_ref.1, bf16[32,256]{1,0:T(8,128)(2,1)} %bitcast.3, bf16[256]{0:T(256)(128)(2,1)} %pre_ref.1, ...), custom_call_target="tpu_custom_call" | custom-call | flops 51539607552 | bytes 62914560 | tf_op jit(solution)/shard_map/pallas_call | solution.py:382
  252.6 1.3 copy.10

commit v5 on v4

--- a/solution.py
+++ b/solution.py
@@ -46,7 +46,7 @@
     experts, capacity,
     h_ref, wg_ref, wu_ref, wd_ref, wr_ref, pre_ref, post_ref, choice_hbm, out_ref,
     choice_ref, hb, wr, pre, post, w0, w1, w2, xn, gates, acc, rbuf, sq_own, sq_far, ob, gb,
-    h_send, h_recv, hf_send, hf_recv, s_send, s_recv, n_send, n_recv, c_sem, w_send, w_recv, w_own, f_send, f_recv,
+    h_send, h_recv, hf_send, hf_recv, s_send, s_recv, n_send, n_recv, c_sem, w_send, w_recv, w_own, f_own, f_send, f_recv,
     r_send, r_recv, q_send, q_recv, o_send, o_recv,
 ):
     num_tok, lw = h_ref.shape
@@ -76,12 +76,11 @@
     pltpu.make_async_copy(choice_hbm, choice_ref, c_sem).start()
 
     barrier = pltpu.get_barrier_semaphore()
-    for df in range(2):
-        for di in range(4):
-            if df or di:
-                pl.semaphore_signal(
-                    barrier, inc=1, device_id={"ffn": (f + df) % 2, "emb": (i + di) % 4}, device_id_type=MESH
-                )
+    for f2, i2 in (
+        (1 - f, 2 * (1 - x) + c), (1 - f, 2 * (1 - x) + 1 - c), (1 - f, i), (1 - f, sib),
+        (f, 2 * (1 - x) + c), (f, 2 * (1 - x) + 1 - c), (f, sib),
+    ):
+        pl.semaphore_signal(barrier, inc=1, device_id={"ffn": f2, "emb": i2}, device_id_type=MESH)
     pl.semaphore_wait(barrier, 7)
 
     def remote(src, dst, send, recv, f2, i2):
@@ -125,22 +124,31 @@
     def group(j):
         return w0.at[j, 0, pl.ds(0, 3 * lw), :]
 
-    def send_expert(j):
-        dst = blocks(j, f, i)
-        e = local_e * q + j
-        for src, to in zip((wg_ref.at[e], wu_ref.at[e], wd_ref.at[e]), dst):
-            pltpu.make_async_copy(src, to, w_own.at[j]).start()
-            remote(src, to, f_send.at[0], f_recv.at[j, 0], f, sib).start()
+    mine = pl.ds(local_e * q, local_e)
+    own_blocks = (
+        w0.at[:, f, rows(i * lw, lw), :],
+        w1.at[:, f, rows(i * lw, lw), :],
+        w2.at[:, i, rows(f * fw, fw), :],
+    )
+    for src, to in zip((wg_ref.at[mine], wu_ref.at[mine], wd_ref.at[mine]), own_blocks):
+        pltpu.make_async_copy(src, to, w_own).start()
+        remote(src, to, f_send.at[0], f_own, f, sib).start()
+
+    def send_block(j, m, d):
+        x2, f2, q2 = chip(d)
+        src = (wg_ref, wu_ref, wd_ref)[m].at[local_e * q2 + j]
+        remote(src, blocks(j, f, i)[m], w_send.at[d - 1], w_recv.at[j, d - 1], f2, 2 * x2 + c).start()
+
+    def send_expert(j, skip=0):
         for m in range(3):
-            for d in (3 - c, 2 + c, 1):
-                x2, f2, q2 = chip(d)
-                e2 = local_e * q2 + j
-                src = (wg_ref.at[e2], wu_ref.at[e2], wd_ref.at[e2])[m]
-                remote(src, dst[m], w_send.at[d - 1], w_recv.at[j, d - 1], f2, 2 * x2 + c).start()
-
-    ahead = 3
+            for d in (3 - c, 2 + c) + (() if m < skip else (1,)):
+                send_block(j, m, d)
+
+    ahead, begun = 3, 2
     for j in range(2):
         send_expert(j)
+    for m in range(begun):
+        send_block(2, m, 1)
 
     await_bytes(choice_ref, c_sem)
 
@@ -176,7 +184,7 @@
         ref = hb.at[e2, across, :]
         remote(ref, ref, hf_send.at[c2], hf_recv.at[c2], 1 - f, i).start()
     for j in range(2, ahead):
-        send_expert(j)
+        send_expert(j, begun if j == 2 else 0)
     for c2 in range(2):
         await_bytes(hb.at[2 * x + c2], h_recv.at[2 * x + c2])
         await_bytes(hb.at[2 * (1 - x) + c2, far, :], hf_recv.at[c2])
@@ -184,6 +192,15 @@
         await_bytes(wr.at[b], s_recv.at[b])
         for n, ref in enumerate((pre, post)):
             await_bytes(ref.at[pl.ds(b * lw, lw)], n_recv.at[n, b])
+
+    def forward(j):
+        for d in (1, 3, 2):
+            x2, f2, _q2 = chip(d)
+            await_bytes(group(j), w_recv.at[j, d - 1])
+            for ref in blocks(j, f2, 2 * x2 + c):
+                remote(ref, ref, f_send.at[d], f_recv.at[j, d - 1], f, sib).start()
+
+    forward(0)
 
     def route(n, _):
         r = rows(n * tile, tile)
@@ -218,6 +235,10 @@
     def along_y(src, slot, t):
         return remote(src, landing(slot, t), r_send.at[slot], r_recv.at[slot, t], 1 - f, i)
 
+    sent = w0.at[pl.ds(0, 3 * local_e // 8)]
+    await_bytes(sent, w_own)
+    await_bytes(sent, f_own)
+
     lane_q = lax.broadcasted_iota(jnp.int32, (quarter, experts), 1)
 
     def expert(j, last):
@@ -226,14 +247,15 @@
             def _():
                 send_expert(j + ahead)
 
-        await_bytes(group(j), w_own.at[j])
+        if last:
+            forward(j)
+        else:
+            @pl.when(j >= 1)
+            def _():
+                forward(j)
+
         for d in (1, 2, 3):
-            x2, f2, _q2 = chip(d)
-            await_bytes(group(j), w_recv.at[j, d - 1])
-            for ref in blocks(j, f2, 2 * x2 + c):
-                remote(ref, ref, f_send.at[d], f_recv.at[j, d], f, sib).start()
-        for d in range(4):
-            await_bytes(group(j), f_recv.at[j, d])
+            await_bytes(group(j), f_recv.at[j, d - 1])
 
         count = 8 if last else 4
         size = half // count
@@ -355,7 +377,6 @@
         await_bytes(hb.at[0, across, :], h_send.at[n])
         await_bytes(hb.at[0, across, :], hf_send.at[n])
 
-    sent = w0.at[pl.ds(0, 3 * local_e // 8)]
     for d in range(4):
         await_bytes(sent, f_send.at[d])
         if d:
@@ -402,8 +423,8 @@
                 pltpu.VMEM((2, 2 * quarter, lw), bf16),
                 pltpu.VMEM((quarter, ffn), bf16),
                 dma((3,)), dma((4,)), dma((2,)), dma((2,)), dma(()), dma((4,)), dma((2,)), dma((2, 4)), dma(()),
-                dma((3,)), dma((local_e, 3)), dma((local_e,)),
-                dma((4,)), dma((local_e, 4)),
+                dma((3,)), dma((local_e, 3)), dma(()), dma(()),
+                dma((4,)), dma((local_e, 3)),
                 dma((3,)), dma((3, 2 * parts)), dma(()), dma((parts,)),
                 dma((3,)), dma((3, parts)),
             ],

time: 254 us -> 253 us (level)
  no operation moved by 1% of the time
where the time goes in v5:
time: 253 us
  Pallas kernels  252 us (100%)
    pallas_call x1, Pallas kernels, local_block(): pl.pallas_call(functools.partial(kernel, experts, capacity), out_shape=pl...  252 us

profile of v5, /device:TPU:0, one launch (start us, length us, event | category | flops | bytes accessed | tf_op | source)
XLA Modules:
  0.0 253.0 jit_solution(11201673043421731551)
XLA Ops:
  0.0 251.7 %shard_map.82 = bf16[4096,256]{1,0:T(8,128)(2,1)S(1)} custom-call(bf16[4096,256]{1,0:T(8,128)(2,1)} %h_ref.1, bf16[32,256,256]{2,1,0:T(8,128)(2,1)} %wg_ref.1, bf16[32,256,256]{2,1,0:T(8,128)(2,1)} %wu_ref.1, bf16[32,256,256]{2,1,0:T(8,128)(2,1)} %wd_ref.1, bf16[32,256]{1,0:T(8,128)(2,1)} %bitcast.3, bf16[256]{0:T(256)(128)(2,1)} %pre_ref.1, ...), custom_call_target="tpu_custom_call" | custom-call | flops 51539607552 | bytes 62914560 | tf_op jit(solution)/shard_map/pallas_call | solution.py:403
  251.7 1.3 copy.10

commit v6 on v5

--- a/solution.py
+++ b/solution.py
@@ -198,7 +198,7 @@
             x2, f2, _q2 = chip(d)
             await_bytes(group(j), w_recv.at[j, d - 1])
             for ref in blocks(j, f2, 2 * x2 + c):
-                remote(ref, ref, f_send.at[d], f_recv.at[j, d - 1], f, sib).start()
+                remote(ref, ref, f_send.at[d], f_recv.at[j], f, sib).start()
 
     forward(0)
 
@@ -254,8 +254,7 @@
             def _():
                 forward(j)
 
-        for d in (1, 2, 3):
-            await_bytes(group(j), f_recv.at[j, d - 1])
+        await_bytes(xn.at[pl.ds(0, 9 * lw * fw // xn.shape[1]), :], f_recv.at[j])
 
         count = 8 if last else 4
         size = half // count
@@ -341,11 +340,11 @@
                 ob[b, s, cols] = (hv + m * inv * gain[:, cols]).astype(bf16)
         for b in range(2):
             remote(
-                ob.at[b, s, :], out_rows(f, c, t), o_send.at[b], o_recv.at[c, t], 1 - f, 2 * x + b
+                ob.at[b, s, :], out_rows(f, c, t), o_send.at[b], o_recv.at[c], 1 - f, 2 * x + b
             ).start()
         own = rows(c * half + f * 2 * quarter + t * part, part)
         out_ref[own, :] = ob[c, s, :]
-        remote(ob.at[1 - c, s, :], out_rows(f, c, t), o_send.at[2], o_recv.at[2, t], f, sib).start()
+        remote(ob.at[1 - c, s, :], out_rows(f, c, t), o_send.at[2], o_recv.at[2], f, sib).start()
 
     for kind, t in REST:
         if kind == "m":
@@ -357,14 +356,8 @@
         else:
             start_piece(kind, t)
 
-    def close(t, _):
-        here = ob.at[0, rows(t * part, part), :]
-        for n in range(3):
-            await_bytes(here, o_recv.at[n, t])
-        return 0
-
-    lax.fori_loop(0, parts, close, 0)
     for n in range(3):
+        await_bytes(ob.at[0], o_recv.at[n])
         await_bytes(ob.at[0], o_send.at[n])
         await_bytes(rbuf.at[0], r_send.at[n])
     await_bytes(sq_own, q_send)
@@ -424,9 +417,9 @@
                 pltpu.VMEM((quarter, ffn), bf16),
                 dma((3,)), dma((4,)), dma((2,)), dma((2,)), dma(()), dma((4,)), dma((2,)), dma((2, 4)), dma(()),
                 dma((3,)), dma((local_e, 3)), dma(()), dma(()),
-                dma((4,)), dma((local_e, 3)),
+                dma((4,)), dma((local_e,)),
                 dma((3,)), dma((3, 2 * parts)), dma(()), dma((parts,)),
-                dma((3,)), dma((3, parts)),
+                dma((3,)), dma((3,)),
             ],
             compiler_params=pltpu.CompilerParams(
                 collective_id=0, has_side_effects=True, vmem_limit_bytes=58 << 20

time: 253 us -> 253 us (level)
  no operation moved by 1% of the time
where the time goes in v6:
time: 253 us
  Pallas kernels  251 us (99%)
    pallas_call x1, Pallas kernels, local_block(): pl.pallas_call(functools.partial(kernel, experts, capacity), out_shape=pl...  251 us

profile of v6, /device:TPU:0, one launch (start us, length us, event | category | flops | bytes accessed | tf_op | source)
XLA Modules:
  0.0 252.7 jit_solution(13318610678734021309)
XLA Ops:
  0.0 251.3 %shard_map.82 = bf16[4096,256]{1,0:T(8,128)(2,1)S(1)} custom-call(bf16[4096,256]{1,0:T(8,128)(2,1)} %h_ref.1, bf16[32,256,256]{2,1,0:T(8,128)(2,1)} %wg_ref.1, bf16[32,256,256]{2,1,0:T(8,128)(2,1)} %wu_ref.1, bf16[32,256,256]{2,1,0:T(8,128)(2,1)} %wd_ref.1, bf16[32,256]{1,0:T(8,128)(2,1)} %bitcast.3, bf16[256]{0:T(256)(128)(2,1)} %pre_ref.1, ...), custom_call_target="tpu_custom_call" | custom-call | flops 51539607552 | bytes 62914560 | tf_op jit(solution)/shard_map/pallas_call | solution.py:396
  251.3 1.3 copy.10

commit v7 on v6

--- a/solution.py
+++ b/solution.py
@@ -47,7 +47,7 @@
     h_ref, wg_ref, wu_ref, wd_ref, wr_ref, pre_ref, post_ref, choice_hbm, out_ref,
     choice_ref, hb, wr, pre, post, w0, w1, w2, xn, gates, acc, rbuf, sq_own, sq_far, ob, gb,
     h_send, h_recv, hf_send, hf_recv, s_send, s_recv, n_send, n_recv, c_sem, w_send, w_recv, w_own, f_own, f_send, f_recv,
-    r_send, r_recv, q_send, q_recv, o_send, o_recv,
+    r_send, r_recv, m_recv, q_send, q_recv, o_send, o_recv,
 ):
     num_tok, lw = h_ref.shape
     fw = wg_ref.shape[2]
@@ -229,11 +229,14 @@
     def landing(slot, t):
         return rbuf.at[slot, t % 2, rows(t // 2 * part, part), :]
 
+    def arrival(slot, t):
+        return m_recv.at[t // 2] if slot else r_recv.at[t]
+
     def along_x(src, slot, t):
-        return remote(src, landing(slot, t), r_send.at[slot], r_recv.at[slot, t], f, 2 * (1 - x) + c)
+        return remote(src, landing(slot, t), r_send.at[slot], arrival(slot, t), f, 2 * (1 - x) + c)
 
     def along_y(src, slot, t):
-        return remote(src, landing(slot, t), r_send.at[slot], r_recv.at[slot, t], 1 - f, i)
+        return remote(src, landing(slot, t), r_send.at[slot], arrival(slot, t), 1 - f, i)
 
     sent = w0.at[pl.ds(0, 3 * local_e // 8)]
     await_bytes(sent, w_own)
@@ -305,16 +308,15 @@
 
     def add_to(xs, fs, t):
         here = piece(xs, fs, t)
-        await_bytes(landing(0, t), r_recv.at[0, t])
+        await_bytes(landing(0, t), r_recv.at[t])
         here[...] = here[...] + landing(0, t)[...]
 
     def total(t):
         r = rows(f * 2 * quarter + t * part, part)
         s = rows(t * part, part)
+        await_bytes(ob.at[0], m_recv.at[t])
         sq = jnp.zeros((part, part), f32)
         for b in range(2):
-            for slot in (1, 2):
-                await_bytes(landing(slot, 2 * t + b), r_recv.at[slot, 2 * t + b])
             v = acc[2 * x + b, r, :] + (rbuf[1, b, s, :] + rbuf[2, b, s, :])
             acc[2 * x + b, r, :] = v
             v = v * v
@@ -418,7 +420,7 @@
                 dma((3,)), dma((4,)), dma((2,)), dma((2,)), dma(()), dma((4,)), dma((2,)), dma((2, 4)), dma(()),
                 dma((3,)), dma((local_e, 3)), dma(()), dma(()),
                 dma((4,)), dma((local_e,)),
-                dma((3,)), dma((3, 2 * parts)), dma(()), dma((parts,)),
+                dma((3,)), dma((2 * parts,)), dma((parts,)), dma(()), dma((parts,)),
                 dma((3,)), dma((3,)),
             ],
             compiler_params=pltpu.CompilerParams(

time: 253 us -> 253 us (level)
  no operation moved by 1% of the time
where the time goes in v7:
time: 253 us; the launch traced here: 252 us
  Pallas kernels  251 us (99%)
    pallas_call x1, Pallas kernels, local_block(): pl.pallas_call(functools.partial(kernel, experts, capacity), out_shape=pl...  251 us

profile of v7, /device:TPU:0, one launch (start us, length us, event | category | flops | bytes accessed | tf_op | source)
XLA Modules:
  0.0 252.4 jit_solution(9886309538148589597)
XLA Ops:
  0.0 251.1 %shard_map.82 = bf16[4096,256]{1,0:T(8,128)(2,1)S(1)} custom-call(bf16[4096,256]{1,0:T(8,128)(2,1)} %h_ref.1, bf16[32,256,256]{2,1,0:T(8,128)(2,1)} %wg_ref.1, bf16[32,256,256]{2,1,0:T(8,128)(2,1)} %wu_ref.1, bf16[32,256,256]{2,1,0:T(8,128)(2,1)} %wd_ref.1, bf16[32,256]{1,0:T(8,128)(2,1)} %bitcast.3, bf16[256]{0:T(256)(128)(2,1)} %pre_ref.1, ...), custom_call_target="tpu_custom_call" | custom-call | flops 51539607552 | bytes 62914560 | tf_op jit(solution)/shard_map/pallas_call | solution.py:398
  251.1 1.3 copy.10
